TPU v7x, 256 devices: a 8x8x2 block of a 8x8x16 slice. The times are simulated.
256 devices in a mesh: grp: 2 (over z), tp: 128 (over x, y, core).
Axes of the slice: x: 8, y: 8, z: 2, core: 2. Of those that a mesh axis runs over, the one named last changes fastest.
The devices are a block of a 8x8x16 slice.
Arguments:
- hidden_in: float32 [64, 4608], P('grp'), parts along dimension 0, may hold values from -6 to 6
- prefill_cache: bfloat16 [128, 1, 2, 4, 128, 8, 256], P('tp', None, None, 'grp'), parts along dimension 3, may hold values from -6 to 6
- lengths: int32 [64], P('grp'), parts along dimension 0, may hold values from 1 to 1023
- page_table: int32 [64, 128], P('grp'), parts along dimension 0, may hold values from 0 to 127, each once within a row
- qkv_weight: bfloat16 [1, 8192, 4608], P(None, 'tp'), may hold values from -0.09375 to 0.09375
- out_weight: bfloat16 [1, 4608, 4096], P(None, 'tp'), may hold values from -0.09375 to 0.09375
- gate_up_weight: bfloat16 [1, 2, 18432, 4608], P(None, None, 'tp'), may hold values from -0.09375 to 0.09375
- down_weight: bfloat16 [1, 18432, 4608], P(None, 'tp'), may hold values from -0.15625 to 0.15625
- norm_gains: float32 [1, 4, 4608], replicated, may hold values from 0.25 to 1.75
Outputs:
- hidden_out: float32 [64, 4608], P('grp', 'tp'), parts along dimension 0
- decode_cache: bfloat16 [128, 1, 2, 64, 8, 2048], P('tp', None, None, 'grp'), parts along dimension 3
There are 2 independent parts, one for each index of `grp`. A program takes and returns all parts, laid end to end along the dimension named above; an argument that names none is the same for every part. Nothing has to cross between parts.
Inputs may be any that keep to these rules, and one draw needn't show every extreme that they name: Request r's new token takes position lengths[r]. Each row is a permutation of 0 to 127; page j of request r holds cache positions page_table[r, j] * 8 to page_table[r, j] * 8 + 7.
All inputs are finite; a program needn't handle non-finite values.
Results may differ from a plain program's by a relative error of at most 0.012.
The roundings to bfloat16 on the way count: a program that leaves them out, or rounds other values in their place, can miss the bound.
Values may be sent and summed in bfloat16 or wider, within the bound.
A program may use at most 64 MiB of HBM per device.

v0:
```python
import jax
import jax.numpy as jnp
from jax import lax
from jax.sharding import Mesh
from jax.sharding import PartitionSpec as P

D = 4608
HEADS = 32
KV_HEADS = 16
HEAD_DIM = 128
PREFILL_TP = 8
TP = ("tp_0", "tp_1", "tp_2")


EPSILON = 1e-06
SOFTCAP = 50.0


def cut_along(shard, dim, size):
    before, after = (shard.shape[:dim], shard.shape[dim + 1 :])
    return jnp.moveaxis(shard.reshape(*before, size, -1, *after), dim, 0)


def joined_along(tiles, dim):
    tiles = jnp.moveaxis(tiles, 0, dim)
    shape = tiles.shape
    return tiles.reshape(*shape[:dim], shape[dim] * shape[dim + 1], *shape[dim + 2 :])


def turned_blocks(tiles, axes, turns):
    shape = [lax.axis_size(a) for a in axes]
    tiles = tiles.reshape(*shape, *tiles.shape[1:])
    for k in turns:
        tiles = lax.all_to_all(tiles, axes[k], split_axis=k, concat_axis=k, tiled=True)
    return tiles.reshape(-1, *tiles.shape[len(axes) :])


def exchange_by_chip(shard, groups, turns, split_dim, concat_dim):
    size = lax.axis_size(groups[0]) * lax.axis_size(groups[1])
    tiles = cut_along(shard, split_dim, size)
    return joined_along(turned_blocks(tiles, groups, turns), concat_dim)


def gather_in_order(shard, axes, turns):
    tiles = shard[None]
    for k in turns:
        tiles = lax.all_gather(tiles, axes[k], axis=0, tiled=True)
    held = [lax.axis_size(axes[k]) for k in reversed(turns)]
    tiles = tiles.reshape(*held, *shard.shape)
    turned = sorted(range(len(turns)), key=lambda place: turns[len(turns) - 1 - place])
    return tiles.transpose(*turned, *range(len(turns), tiles.ndim)).reshape(-1, *shard.shape)


def gather_axes(shard, axes, turns, dim):
    return joined_along(gather_in_order(shard, axes, turns), dim)


def own_block(tiles, axes, turns):
    shape = [lax.axis_size(a) for a in axes]
    tiles = tiles.reshape(*shape, *tiles.shape[1:])
    tiles = tiles.transpose(*turns, *range(len(axes), tiles.ndim))
    tiles = tiles.reshape(-1, *tiles.shape[len(axes) :])
    for k in turns:
        tiles = lax.psum_scatter(tiles, axes[k], scatter_dimension=0, tiled=True)
    return tiles[0]


def summed_rows(shard, axes, turns, dim):
    size = lax.axis_size(axes)
    return own_block(cut_along(shard, dim, size), axes, turns)


def one_axis_at_a_time(shard, axes):
    for axis in axes:
        shard = lax.psum(shard, axis)
    return shard


def rms_scale(vector, gain_row):
    meansq = jnp.mean(vector * vector, axis=-1, keepdims=True)
    return vector * lax.rsqrt(meansq + EPSILON) * (1.0 + gain_row)


def rotate(vector, positions):
    half_dim = vector.shape[-1] // 2
    exponent = jnp.arange(half_dim, dtype=jnp.float32) * (-2.0 / vector.shape[-1])
    frequency = jnp.power(jnp.float32(10000.0), exponent)
    angles = positions.astype(jnp.float32)[:, None, None] * frequency
    cosine = jnp.cos(angles)
    sine_term = jnp.sin(angles)
    front_half = vector[..., :half_dim]
    back_half = vector[..., half_dim:]
    return jnp.concatenate(
        [front_half * cosine - back_half * sine_term, back_half * cosine + front_half * sine_term],
        axis=-1,
    )


def capped(raw_scores):
    return SOFTCAP * jnp.tanh(raw_scores / SOFTCAP)


def round_back(vector):
    return lax.optimization_barrier(vector.astype(jnp.bfloat16)).astype(jnp.float32)


def pick_slot(vector, my_group, my_slot):
    inner = lax.dynamic_index_in_dim(vector, my_group, 0, False)
    return lax.dynamic_index_in_dim(inner, my_slot, 1, False)


def take_pages(page_block, page_order):
    return jnp.take(page_block, page_order, axis=2)


def project_rows(left, weight_rows):
    return jnp.einsum("bd,cd->bc", left, weight_rows, preferred_element_type=jnp.float32)


def on_device(
    hidden_in,
    prefill_cache,
    lengths,
    page_table,
    qkv_weight,
    out_weight,
    gate_up_weight,
    down_weight,
    norm_gains,
):
    devices = lax.axis_size(TP)
    my_index = lax.axis_index(TP)
    batch_rows = hidden_in.shape[0]
    groups = devices // PREFILL_TP
    per_group = batch_rows // groups
    local_heads = KV_HEADS // PREFILL_TP
    head_share = HEADS // KV_HEADS
    layer_count = prefill_cache.shape[1]
    page_width = prefill_cache.shape[5]
    score_scale = (D / HEADS) ** (-0.5)
    q_cols = HEADS * HEAD_DIM
    k_cols = KV_HEADS * HEAD_DIM
    my_group = my_index // PREFILL_TP
    my_slot = my_index % PREFILL_TP
    group_rows = lax.dynamic_slice_in_dim(page_table, my_group * per_group, per_group, 0)
    group_lengths = lax.dynamic_slice_in_dim(lengths, my_group * per_group, per_group, 0)
    local_cache = prefill_cache[0]
    page_ids = jnp.arange(devices, dtype=jnp.int32)
    onehot = (group_rows[:, :, None] == page_ids[None, None, :]).astype(jnp.int32)
    inverse = jnp.sum(onehot * page_ids[None, :, None], axis=1)
    arranged = jax.vmap(take_pages, in_axes=(2, 0), out_axes=2)(local_cache, inverse)
    relaid = exchange_by_chip(arranged, (("tp_0", "tp_1"), "tp_2"), (1, 0), 3, 3)
    relaid = relaid.reshape(
        layer_count, 2, per_group, groups, PREFILL_TP, page_width, local_heads, HEAD_DIM
    )
    decode_local = relaid.transpose(0, 1, 3, 2, 5, 4, 6, 7).reshape(
        layer_count, 2, batch_rows, page_width, k_cols
    )
    my_pos = my_index * page_width + jnp.arange(page_width, dtype=jnp.int32)
    fresh_slot = my_pos[None, :] == lengths[:, None]
    kept_cache = local_cache.reshape(
        layer_count, 2, per_group, devices, page_width, local_heads, HEAD_DIM
    )
    cache_pos = (
        group_rows[:, :, None] * page_width + jnp.arange(page_width, dtype=jnp.int32)[None, None, :]
    )
    kept_visible = cache_pos < group_lengths[:, None, None]
    stream = hidden_in
    normed = rms_scale(stream, norm_gains[0, 0]).astype(jnp.bfloat16)
    column_part = project_rows(normed, qkv_weight[0]).astype(jnp.bfloat16)
    projected = gather_axes(column_part, (("tp_0", "tp_1"), "tp_2"), (0, 1), 1)
    queries = rotate(
        projected[:, :q_cols].astype(jnp.float32).reshape(batch_rows, HEADS, HEAD_DIM), lengths
    ).astype(jnp.bfloat16)
    new_key = rotate(
        projected[:, q_cols : q_cols + k_cols]
        .astype(jnp.float32)
        .reshape(batch_rows, KV_HEADS, HEAD_DIM),
        lengths,
    ).astype(jnp.bfloat16)
    new_value = projected[:, q_cols + k_cols :]
    key_layer = jnp.where(
        fresh_slot[:, :, None], new_key.reshape(batch_rows, 1, k_cols), decode_local[0, 0]
    )
    value_layer = jnp.where(
        fresh_slot[:, :, None], new_value.reshape(batch_rows, 1, k_cols), decode_local[0, 1]
    )
    written = [jnp.stack([key_layer, value_layer], axis=0)]
    flat_q = queries.reshape(batch_rows, KV_HEADS, head_share, HEAD_DIM)
    flat_k = new_key.reshape(batch_rows, KV_HEADS, 1, HEAD_DIM)
    flat_v = new_value.reshape(batch_rows, KV_HEADS, 1, HEAD_DIM)
    own_weight = jnp.exp(
        capped(
            jnp.sum(flat_q.astype(jnp.float32) * flat_k.astype(jnp.float32), axis=-1) * score_scale
        )
    )
    own_term = round_back(own_weight)[..., None] * flat_v.astype(jnp.float32)
    shaped_q = flat_q.reshape(groups, per_group, PREFILL_TP, local_heads, head_share, HEAD_DIM)
    shaped_own = own_weight.reshape(groups, per_group, PREFILL_TP, local_heads, head_share)
    shaped_term = own_term.reshape(groups, per_group, PREFILL_TP, local_heads, head_share, HEAD_DIM)
    my_queries = pick_slot(shaped_q, my_group, my_slot)
    cached_keys = kept_cache[0, 0]
    cached_values = kept_cache[0, 1]
    raw_scores = (
        jnp.einsum("ramd,rjcad->ramjc", my_queries, cached_keys, preferred_element_type=jnp.float32)
        * score_scale
    )
    weights = jnp.where(kept_visible[:, None, None, :, :], jnp.exp(capped(raw_scores)), 0.0)
    numerator = jnp.einsum(
        "ramjc,rjcad->ramd",
        weights.astype(jnp.bfloat16),
        cached_values,
        preferred_element_type=jnp.float32,
    )
    numerator = numerator + pick_slot(shaped_term, my_group, my_slot)
    denominator = jnp.sum(weights, axis=(-2, -1)) + pick_slot(shaped_own, my_group, my_slot)
    mine = (
        (numerator / denominator[..., None])
        .astype(jnp.bfloat16)
        .reshape(1, per_group, local_heads * head_share * HEAD_DIM)
    )
    gathered = lax.all_gather(mine, TP, axis=0, tiled=True)
    attended = (
        gathered.reshape(groups, PREFILL_TP, per_group, local_heads * head_share * HEAD_DIM)
        .transpose(0, 2, 1, 3)
        .reshape(batch_rows, q_cols)
    )
    mixed_part = project_rows(attended, out_weight[0]).astype(jnp.bfloat16)
    mixed_out = gather_axes(mixed_part, (("tp_0", "tp_1"), "tp_2"), (0, 1), 1)
    stream = stream + rms_scale(mixed_out.astype(jnp.float32), norm_gains[0, 1])
    ffn_in = rms_scale(stream, norm_gains[0, 2]).astype(jnp.bfloat16)
    gate_proj = project_rows(ffn_in, gate_up_weight[0, 0])
    up_proj = project_rows(ffn_in, gate_up_weight[0, 1])
    active = (jax.nn.gelu(gate_proj, approximate=True) * up_proj).astype(jnp.bfloat16)
    branch = jnp.dot(active, down_weight[0], preferred_element_type=jnp.float32)
    column_count = branch.shape[1] // devices
    portion = summed_rows(branch.astype(jnp.bfloat16), TP, (2, 0, 1), 1).astype(jnp.float32)
    squares = one_axis_at_a_time(jnp.sum(portion * portion, axis=-1), TP)
    gain_part = lax.dynamic_slice_in_dim(norm_gains[0, 3], my_index * column_count, column_count, 0)
    stream_part = lax.dynamic_slice_in_dim(stream, my_index * column_count, column_count, 1)
    result = stream_part + portion * lax.rsqrt(squares[:, None] / D + EPSILON) * (1.0 + gain_part)
    decode_cache = jnp.stack(written, axis=0)[None]
    return (result, decode_cache)


def solution(mesh):
    torus = Mesh(mesh.devices.reshape(mesh.shape["grp"], 8, 8, 2), ("grp", "tp_0", "tp_1", "tp_2"))
    return jax.shard_map(
        on_device,
        mesh=torus,
        in_specs=(
            P("grp", None),
            P(TP, None, None, "grp", None, None, None),
            P("grp"),
            P("grp", None),
            P(None, TP, None),
            P(None, TP, None),
            P(None, None, TP, None),
            P(None, TP, None),
            P(),
        ),
        out_specs=(P("grp", TP), P(TP, None, None, "grp", None, None)),
        check_vma=False,
    )
```

profile of v0, /device:TPU:513, one launch (start us, length us, event | category | flops | bytes accessed | tf_op | source)
XLA Modules:
  0.0 438.4 jit_solution(14225029123569597473)
XLA Ops:
  7.2 0.8 broadcast_multiply_fusion
  8.0 0.1 select_reduce_fusion
  8.2 2.8 gather_fusion
  10.9 0.5 broadcast_select_fusion
  11.4 0.1 copy.124
  11.5 25.5 %all_to_all.10 = bf16[64,2,1,2,2,1,8,256]{7,6,0,4,3,5,2,1:T(8,128)(2,1)S(1)} all-to-all(bf16[64,2,1,2,2,1,8,256]{7,6,0,4,3,5,2,1:T(8,128)(2,1)S(1)} %copy.124), channel_id=1, replica_groups=mesh['grp'=2,'tp_0'=8,'tp_1'=8,'tp_2'=2] {'tp_2'}, dimensions={1} | all-to-all | bytes 4194304 | tf_op jit(solution)/shard_map/all_to_all | solution.py:34
  37.0 1.6 copy.125
  38.6 7.3 %all-to-all-start.1 = ((bf16[64,2,1,2,2,1,8,256]{7,6,1,4,3,5,2,0:T(8,128)(2,1)}), bf16[64,2,1,2,2,1,8,256]{7,6,1,4,3,5,2,0:T(8,128)(2,1)}, u32[]{:S(2)}, u32[]{:S(2)}) async-start(bf16[64,2,1,2,2,1,8,256]{7,6,1,4,3,5,2,0:T(8,128)(2,1)} %copy.125), calls=%async_computation.4 | async-start | bytes 4194304 | tf_op jit(solution)/shard_map/all_to_all | solution.py:34
  46.1 1.3 add_reduce_fusion
  47.4 0.2 multiply_reduce_fusion.1
  47.6 0.3 convolution_convert_fusion.1
  47.9 83.7 %all-gather = bf16[2048,64]{1,0:T(8,128)(2,1)S(1)} all-gather(bf16[32,64]{1,0:T(8,128)(2,1)S(1)} %convolution_convert_fusion.1), channel_id=2, replica_groups=mesh['grp'=2,'tp_0'=8,'tp_1'=8,'tp_2'=2] {'tp_0','tp_1'}, dimensions={0}, use_global_device_ids=true | all-gather | bytes 266240 | tf_op jit(solution)/shard_map/all_gather | solution.py:47
  131.7 13.7 %all_gather.16 = bf16[128,32,64]{2,1,0:T(8,128)(2,1)S(1)} all-gather(bf16[64,32,64]{2,1,0:T(8,128)(2,1)S(1)} %bitcast.167), channel_id=1, replica_groups=mesh['grp'=2,'tp_0'=8,'tp_1'=8,'tp_2'=2] {'tp_2'}, dimensions={0}, use_global_device_ids=true | all-gather | bytes 786432 | tf_op jit(solution)/shard_map/all_gather | solution.py:47
  145.4 1.1 copy.130
  146.5 1.3 copy.111
  147.9 1.4 copy.112
  149.3 2.9 reshape.346
  152.1 1.8 convert_bitcast_fusion.1
  153.9 1.8 fusion.55
  155.7 1.7 fusion.54
  157.4 1.1 copy.135
  158.5 1.2 reshape.367
  159.7 1.0 copy.136
  160.7 0.1 multiply_cosine_fusion
  160.9 0.2 add_convert_fusion
  161.1 0.2 multiply_subtract_fusion
  161.3 0.8 fusion.53
  162.1 1.3 multiply_reduce_fusion.2
  163.4 0.2 copy.115
  163.6 0.2 reshape.366
  163.8 2.3 copy.116
  166.1 0.2 exp.12
  166.5 0.5 fusion.56
  167.0 0.7 constant_dynamic-slice_fusion
  167.7 1.5 fusion.22
  169.2 47.3 %all_gather.17 = bf16[128,2,512]{2,1,0:T(2,128)(2,1)S(1)} all-gather(bf16[1,2,512]{2,1,0:T(2,128)(2,1)S(1)} %reshape.351), channel_id=1, replica_groups=mesh['grp'=2,'tp_0'=8,'tp_1'=8,'tp_2'=2] {'tp_0','tp_1','tp_2'}, dimensions={0}, use_global_device_ids=true | all-gather | bytes 264192 | tf_op jit(solution)/shard_map/all_gather | solution.py:222
  216.7 0.2 convolution_convert_fusion.2
  216.9 38.2 %all-gather.1 = bf16[2048,36]{1,0:T(8,128)(2,1)S(1)} all-gather(bf16[32,36]{1,0:T(8,128)(2,1)S(1)} %convolution_convert_fusion.2), channel_id=3, replica_groups=mesh['grp'=2,'tp_0'=8,'tp_1'=8,'tp_2'=2] {'tp_0','tp_1'}, dimensions={0}, use_global_device_ids=true | all-gather | bytes 149760 | tf_op jit(solution)/shard_map/all_gather | solution.py:47
  255.2 14.1 %all_gather.19 = bf16[128,32,36]{2,1,0:T(8,128)(2,1)S(1)} all-gather(bf16[64,32,36]{2,1,0:T(8,128)(2,1)S(1)} %bitcast.168), channel_id=1, replica_groups=mesh['grp'=2,'tp_0'=8,'tp_1'=8,'tp_2'=2] {'tp_2'}, dimensions={0}, use_global_device_ids=true | all-gather | bytes 442368 | tf_op jit(solution)/shard_map/all_gather | solution.py:47
  269.2 0.3 convert_bitcast_fusion
  269.5 2.9 copy.121
  272.5 3.3 reshape.368
  275.7 0.4 fusion
  276.2 1.2 multiply_reduce_fusion
  277.5 0.6 fusion.35
  278.1 2.5 convolution_convert_fusion
  280.6 2.8 reshape.355
  283.4 1.6 copy.122
  285.2 16.1 %reduce-scatter.4.cloned.1.call-done = bf16[64,32,36]{2,1,0:T(8,128)(2,1)} async-done(((bf16[128,32,36]{2,1,0:T(8,128)(2,1)}), bf16[64,32,36]{2,1,0:T(8,128)(2,1)}) %reduce-scatter.4.cloned.1.call-update) | async-done | bytes 147472 | tf_op jit(solution)/shard_map/reduce_scatter | solution.py:64
  301.5 0.7 broadcast_compare_fusion
  302.2 35.5 %reduce-scatter.6.cloned.1.call-done = bf16[8,32,36]{2,1,0:T(8,128)(2,1)} async-done(((bf16[64,32,36]{2,1,0:T(8,128)(2,1)}), bf16[8,32,36]{2,1,0:T(8,128)(2,1)}) %reduce-scatter.6.cloned.1.call-update) | async-done | bytes 18448 | tf_op jit(solution)/shard_map/reduce_scatter | solution.py:64
  337.7 0.8 fusion.50
  338.4 0.7 copy.150
  339.1 38.0 %reduce-scatter.8.cloned.1.call-done = bf16[1,32,36]{2,1,0:T(8,128)(2,1)} async-done(((bf16[8,32,36]{2,1,0:T(8,128)(2,1)}), bf16[1,32,36]{2,1,0:T(8,128)(2,1)}) %reduce-scatter.8.cloned.1.call-update) | async-done | bytes 2320 | tf_op jit(solution)/shard_map/reduce_scatter | solution.py:64
  377.2 0.8 fusion.38
  378.0 13.2 %psum.21 = f32[32]{0:T(128)S(1)} all-reduce(f32[32]{0:T(128)S(1)} %fusion.38), channel_id=1, replica_groups=mesh['grp'=2,'tp_0'=8,'tp_1'=8,'tp_2'=2] {'tp_0'}, use_global_device_ids=true, to_apply=%region_9.10 | all-reduce | flops 32 | bytes 256 | tf_op jit(solution)/shard_map/psum | solution.py:75
  391.1 12.0 %psum.22 = f32[32]{0:T(128)S(1)} all-reduce(f32[32]{0:T(128)S(1)} %psum.21), channel_id=1, replica_groups=mesh['grp'=2,'tp_0'=8,'tp_1'=8,'tp_2'=2] {'tp_1'}, use_global_device_ids=true, to_apply=%region_10.11 | all-reduce | flops 32 | bytes 256 | tf_op jit(solution)/shard_map/psum | solution.py:75
  403.1 15.9 %psum.23 = f32[32]{0:T(128)S(1)} all-reduce(f32[32]{0:T(128)S(1)} %psum.22), channel_id=1, replica_groups=mesh['grp'=2,'tp_0'=8,'tp_1'=8,'tp_2'=2] {'tp_2'}, use_global_device_ids=true, to_apply=%region_11.12 | all-reduce | flops 32 | bytes 256 | tf_op jit(solution)/shard_map/psum | solution.py:75
  419.1 1.4 fusion.40
  420.5 1.8 copy.126
  422.2 3.5 copy.127
  425.8 3.3 reshape.361
  429.1 1.2 fusion.24
  430.4 1.5 maximum_bitcast_fusion
  (57 shorter events, 1.0 us)
Async XLA Ops:
  7.2 270.9 %copy-start = (bf16[1,144,4608]{2,1,0:T(8,128)(2,1)S(1)}, bf16[1,144,4608]{2,1,0:T(8,128)(2,1)}, u32[]{:S(2)}) copy-start(bf16[1,144,4608]{2,1,0:T(8,128)(2,1)} %param.16) | copy-start | bytes 3981316
  38.6 7.5 %copy-start.13 = (s32[32]{0:T(128)S(1)}, s32[32]{0:T(128)}, u32[]{:S(2)}) copy-start(s32[32]{0:T(128)} %param.11) | copy-start | bytes 388
  38.6 7.6 %copy-start.12 = (f32[1,4,4608]{2,1,0:T(4,128)S(1)}, f32[1,4,4608]{2,1,0:T(4,128)}, u32[]{:S(2)}) copy-start(f32[1,4,4608]{2,1,0:T(4,128)} %param.17) | copy-start | bytes 221188
  38.6 8.8 %copy-start.2 = (f32[32,4608]{1,0:T(8,128)S(1)}, f32[32,4608]{1,0:T(8,128)}, u32[]{:S(2)}) copy-start(f32[32,4608]{1,0:T(8,128)} %param.9) | copy-start | bytes 1769476
  38.6 9.0 %copy-start.6 = (bf16[1,64,4608]{2,1,0:T(8,128)(2,1)S(1)}, bf16[1,64,4608]{2,1,0:T(8,128)(2,1)}, u32[]{:S(2)}) copy-start(bf16[1,64,4608]{2,1,0:T(8,128)(2,1)} %param.13) | copy-start | bytes 1769476
  38.6 381.9 %all-to-all-start.1 = ((bf16[64,2,1,2,2,1,8,256]{7,6,1,4,3,5,2,0:T(8,128)(2,1)}), bf16[64,2,1,2,2,1,8,256]{7,6,1,4,3,5,2,0:T(8,128)(2,1)}, u32[]{:S(2)}, u32[]{:S(2)}) async-start(bf16[64,2,1,2,2,1,8,256]{7,6,1,4,3,5,2,0:T(8,128)(2,1)} %copy.125), calls=%async_computation.4 | async-start | bytes 4194304 | tf_op jit(solution)/shard_map/all_to_all | solution.py:34
  45.9 255.4 %reduce-scatter.4.cloned.1.call-start = ((), (), s32[]{:S(2)}) async-start(), calls=%async_computation.5 | async-start | bytes 1572864 | tf_op jit(solution)/shard_map/reduce_scatter | solution.py:64
  149.2 6.5 %copy-start.1 = (bf16[1,1,2,2,128,8,256]{6,5,4,3,2,1,0:T(8,128)(2,1)S(1)}, bf16[1,1,2,2,128,8,256]{6,5,4,3,2,1,0:T(8,128)(2,1)}, u32[]{:S(2)}) copy-start(bf16[1,1,2,2,128,8,256]{6,5,4,3,2,1,0:T(8,128)(2,1)} %param.10) | copy-start | bytes 6291460
  161.1 5.4 %copy-start.4 = (bf16[1,1,2,128,8,2,128]{6,4,5,3,2,1,0:T(8,128)(2,1)S(1)}, bf16[1,1,2,128,8,2,128]{6,4,5,3,2,1,0:T(8,128)(2,1)}, u32[]{:S(2)}) copy-start(bf16[1,1,2,128,8,2,128]{6,4,5,3,2,1,0:T(8,128)(2,1)} %get-tuple-element.13) | copy-start | bytes 3145732
  166.5 50.2 %copy-start.9 = (bf16[1,36,4096]{2,1,0:T(8,128)(2,1)S(1)}, bf16[1,36,4096]{2,1,0:T(8,128)(2,1)}, u32[]{:S(2)}) copy-start(bf16[1,36,4096]{2,1,0:T(8,128)(2,1)} %param.14) | copy-start | bytes 884740
  272.5 3.7 copy-start.3
  275.7 1.8 copy-start.5
  275.7 1.8 copy-start.10
  276.2 1.9 copy-start.11
  283.4 18.1 %copy-start.14 = (s32[32]{0:T(128)S(1)}, s32[32]{0:T(128)}, u32[]{:S(2)}) copy-start(s32[32]{0:T(128)} %param.11) | copy-start | bytes 388
  283.4 55.0 %copy-start.8 = (bf16[32,16,128]{2,1,0:T(8,128)(2,1)S(1)}, bf16[32,16,128]{2,1,0:T(8,128)(2,1)}, u32[]{:S(2)}) copy-start(bf16[32,16,128]{2,1,0:T(8,128)(2,1)} %get-tuple-element.8) | copy-start | bytes 393220
  285.1 52.5 %reduce-scatter.6.cloned.1.call-start = ((), (), s32[]{:S(2)}) async-start(), calls=%async_computation.6 | async-start | bytes 589824 | tf_op jit(solution)/shard_map/reduce_scatter | solution.py:64
  301.4 75.7 %reduce-scatter.8.cloned.1.call-start = ((), (), s32[]{:S(2)}) async-start(), calls=%async_computation.7 | async-start | bytes 73728 | tf_op jit(solution)/shard_map/reduce_scatter | solution.py:64
  425.8 3.3 copy-start.7
Sparse Core Ops, SparseCore 0:
  285.3 16.0 reduce-scatter.3
  303.9 33.6 reduce-scatter.5
  340.1 36.9 reduce-scatter.7
where the time goes:
time: 439 us; the launch traced here: 438 us
  blocking collectives  264 us (60%)
  waiting for transfers between devices  89.8 us (20%)
  local copies, waits for them, and re-layouts  40.1 us (9%)
  other arithmetic  17.5 us (4%)
  between operations  14.2 us (3%)
  starting transfers between devices  7.52 us (2%)
  matrix products  5.66 us (1%)
    all_gather x4, blocking collectives, gather_in_order(): tiles = lax.all_gather(tiles, axes[k], axis=0, tiled=True)  150 us
    reduce_scatter x3, waiting for transfers between devices, own_block(): tiles = lax.psum_scatter(tiles, axes[k], scatter_dimension=0, tiled=True)  89.6 us
    all_gather x1, blocking collectives, on_device(): gathered = lax.all_gather(mine, TP, axis=0, tiled=True)  47.3 us
    psum x3, blocking collectives, one_axis_at_a_time(): shard = lax.psum(shard, axis)  41.1 us
    all_to_all x1, blocking collectives, turned_blocks(): lax.all_to_all(tiles, axes[k], split_axis=k, concat_axis=k, tiled=True)  25.5 us
  transfers between devices with their start and end apart: 4, of which 3 were waited for; matrix products, arithmetic and copies ran while one was open for 10% of the time, Pallas kernels for 0%

commit v1 on v0

v1 whole, which is shorter than its diff:
```python
import jax
import jax.numpy as jnp
from jax import lax
from jax.experimental import pallas as pl
from jax.experimental.pallas import tpu as pltpu
from jax.sharding import Mesh
from jax.sharding import PartitionSpec as P

D = 4608
HEADS = 32
KV_HEADS = 16
HEAD_DIM = 128
PREFILL_TP = 8
NX, NY, NC = 8, 8, 2
CHIPS = NX * NY
GROUP = CHIPS * NC
COLS = D // GROUP
TILE = 128
TILES = D // TILE
TP = ("tp_0", "tp_1", "tp_2")
MESH = pl.DeviceIdType.MESH
BF16 = jnp.bfloat16
F32 = jnp.float32

EPSILON = 1e-06
SOFTCAP = 50.0

A2A_POINTS = (16, 34, 50, 66, 84, 100, 116, 127)


def capped(raw_scores):
    return SOFTCAP * jnp.tanh(raw_scores / SOFTCAP)


def rms_scale(vector, gain_row):
    meansq = jnp.mean(vector * vector, axis=-1, keepdims=True)
    return vector * lax.rsqrt(meansq + EPSILON) * (1.0 + gain_row)


def dot_t(left, right):
    return lax.dot_general(left, right, (((1,), (1,)), ((), ())), preferred_element_type=F32)


def dot_n(left, right):
    return jnp.dot(left, right, preferred_element_type=F32)


def step_kernel(
    inv_ref, vis_ref, cos_ref, sin_ref, hid_hbm, paged_hbm, cache_hbm, wq_hbm, wo_hbm, wg_hbm, wd_hbm, gain_hbm,
    res_ref, nk_ref, nv_ref, dec_ref,
    hid, paged, cache, wq, wo, wg, wd, gain, arr, qs, qr, att_buf, att, mix_buf, mix, stream,
    br, pr, sb, rs_buf, fin, in_sem, own_sem, ss, rs,
):
    grp = lax.axis_index("grp")
    x = lax.axis_index("tp_0")
    y = lax.axis_index("tp_1")
    c = lax.axis_index("tp_2")
    chip = x * NY + y
    me = chip * NC + c
    my_group = lax.div(me, PREFILL_TP)
    my_slot = lax.rem(me, PREFILL_TP)

    def at(tx, ty, tc):
        return (grp, tx, ty, tc)

    barrier = pltpu.get_barrier_semaphore()

    def peer(i):
        tx = lax.rem(x + lax.div(i, NY * NC), NX)
        ty = lax.rem(y + lax.rem(lax.div(i, NC), NY), NY)
        tc = lax.rem(c + lax.rem(i, NC), NC)
        return tx, ty, tc

    def greet(i, carry):
        pl.semaphore_signal(barrier, inc=1, device_id=at(*peer(i)), device_id_type=MESH)
        return carry

    loads = [
        (hid_hbm, hid), (gain_hbm.at[0], gain), (wq_hbm.at[0], wq), (paged_hbm, paged),
        (wo_hbm.at[0], wo), (wg_hbm.at[0], wg), (wd_hbm.at[0], wd), (cache_hbm, cache),
    ]
    copies = [pltpu.make_async_copy(s, d, in_sem.at[n]) for n, (s, d) in enumerate(loads)]
    for copy in copies:
        copy.start()
    lax.fori_loop(1, GROUP, greet, 0)

    def send(src, dst, phase, target):
        pltpu.make_async_remote_copy(
            src_ref=src, dst_ref=dst, send_sem=ss.at[phase], recv_sem=rs.at[phase],
            device_id=target, device_id_type=MESH,
        ).start()

    def take(ref, sem):
        pltpu.make_async_copy(ref, ref, sem).wait()

    dec_mine = dec_ref.at[0, 0, :, pl.ds(my_group * 2, 2), :, pl.ds(pl.multiple_of(my_slot * 256, 256), 256)]

    def send_pages(first, last):
        def body(j, carry):
            tx, ty, tc = peer(lax.rem(j * 37, GROUP))
            send(arr.at[(tx * NY + ty) * NC + tc], dec_mine, 0, at(tx, ty, tc))
            return carry

        lax.fori_loop(first, last, body, 0)

    starts = (1,) + tuple(p + 1 for p in A2A_POINTS[:-1])
    stops = tuple(p + 1 for p in A2A_POINTS)

    def pages(n):
        send_pages(starts[n], stops[n])

    def spread(buf, phase):
        def body(i, carry):
            tx = lax.rem(x + lax.div(i, NY), NX)
            ty = lax.rem(y + lax.rem(i, NY), NY)
            send(buf.at[c, chip], buf.at[c, chip], phase, at(tx, ty, c))
            return carry

        lax.fori_loop(1, CHIPS, body, 0)

    def swap(buf, phase):
        send(buf.at[c], buf.at[c], phase, at(x, y, 1 - c))

    copies[0].wait()
    copies[1].wait()
    normed = rms_scale(hid[...], gain[0:1, :]).astype(BF16)
    copies[2].wait()
    part = dot_t(normed, wq[...]).astype(BF16).astype(F32)
    qs[...] = jnp.concatenate([part, part], axis=1).reshape(4, 8, TILE)

    copies[3].wait()

    def arrange(q, carry):
        for e in range(2):
            page = inv_ref[e, q]
            for kv in range(2):
                arr[q, kv, e] = paged[kv, e, page]
        return carry

    lax.fori_loop(0, GROUP, arrange, 0, unroll=4)
    pl.semaphore_wait(barrier, GROUP - 1)

    is_kv = lax.div(x, 4)
    xx = lax.rem(x, 2)
    ty4 = (1 - is_kv) * x + is_kv * (xx * 2 + lax.div(y, 4))
    tc4 = (1 - is_kv) * lax.div(y, 4) + is_kv * lax.rem(lax.div(y, 2), 2)
    slot = (1 - is_kv) * (lax.rem(y, 4) * 2 + c) + is_kv * (
        8 + lax.div(lax.rem(x, 4), 2) * 4 + lax.rem(y, 2) * 2 + c
    )

    def send_heads(i, carry):
        tx = lax.rem(x + lax.div(i, 2), NX)
        ty = ty4 + 4 * lax.rem(i, 2)
        mine = (tx == x) & (ty == y) & (tc4 == c)

        @pl.when(jnp.logical_not(mine))
        def _():
            send(qs.at[lax.div(tx, 2)], qr.at[slot], 1, at(tx, ty, tc4))

        @pl.when(mine)
        def _():
            qr[slot] = qs[lax.div(tx, 2)]

        return carry

    lax.fori_loop(0, 16, send_heads, 0)
    keeps_one = (lax.rem(y, 4) == ty4) & (tc4 == c)
    own_copy = pltpu.make_async_copy(arr.at[me], dec_mine, own_sem.at[0])
    own_copy.start()
    pages(0)

    @pl.when(keeps_one)
    def _():
        take(qr.at[pl.ds(0, 15)], rs.at[1])

    @pl.when(jnp.logical_not(keeps_one))
    def _():
        take(qr.at[pl.ds(0, 16)], rs.at[1])

    copies[7].wait()

    lane = lax.broadcasted_iota(jnp.int32, (8, TILE), 1)
    rows8 = lax.broadcasted_iota(jnp.int32, (8, TILE), 0)
    rows16 = lax.broadcasted_iota(jnp.int32, (16, TILE), 0)
    scale = (D / HEADS) ** (-0.5)
    message = jnp.zeros((16, TILE), F32)
    row0 = lax.rem(my_group, 4) * 2
    for e in range(2):
        cos = jnp.broadcast_to(cos_ref[e : e + 1, :], (8, TILE))
        sin = jnp.broadcast_to(sin_ref[e : e + 1, :], (8, TILE))

        def head(i):
            low = jnp.broadcast_to(qr[2 * i, pl.ds(row0 + e, 1), :], (8, TILE))
            high = jnp.broadcast_to(qr[2 * i + 1, pl.ds(row0 + e, 1), :], (8, TILE))
            return jnp.where(lane < HEAD_DIM // 2, low, high)

        def turned(u):
            return (u * cos + pltpu.roll(u, HEAD_DIM // 2, 1) * sin).astype(BF16).astype(F32)

        q = [turned(head(i)) for i in range(4)]
        k = [turned(head(4 + a)) for a in range(2)]
        v = [head(6 + a) for a in range(2)]
        zero = jnp.zeros((8, TILE), F32)
        left = jnp.where(rows8 == 0, q[0], jnp.where(rows8 == 1, q[1], zero))
        right = jnp.where(rows8 == 2, q[2], jnp.where(rows8 == 3, q[3], zero))
        own_raw = jnp.sum(left * k[0] + right * k[1], axis=1, keepdims=True) * scale
        own = jnp.exp(capped(own_raw))
        both = jnp.concatenate([left, right], axis=1).astype(BF16)
        raw = dot_t(both, cache[0, e]) * scale
        seen = jnp.broadcast_to(vis_ref[e : e + 1, :], raw.shape)
        weights = jnp.where(seen > 0.5, jnp.exp(capped(raw)), 0.0)
        den = jnp.sum(weights, axis=1, keepdims=True) + own
        num = dot_n(weights.astype(BF16), cache[1, e])
        own_b = own.astype(BF16).astype(F32)
        out_l = (num[:, :TILE] + own_b * v[0]) / den
        out_r = (num[:, TILE:] + own_b * v[1]) / den
        rows = [out_l[0:1], out_l[1:2], out_r[2:3], out_r[3:4], k[0][0:1], k[1][0:1], v[0][0:1], v[1][0:1]]
        for j, row in enumerate(rows):
            message = jnp.where(rows16 == e * 8 + j, jnp.broadcast_to(row, (16, TILE)), message)
    att_buf[c, chip] = message.astype(BF16)

    spread(att_buf, 2)
    pages(1)
    take(att_buf.at[0, pl.ds(0, CHIPS - 1)], rs.at[2])
    swap(att_buf, 3)
    take(att_buf.at[0], rs.at[3])

    want = lax.broadcasted_iota(jnp.int32, (128, 256), 0)
    have = lax.broadcasted_iota(jnp.int32, (128, 256), 1)
    target = 8 * lax.rem(want, 32) + lax.div(want, 32)
    pick_q = jnp.where(have == target, 1.0, 0.0).astype(BF16)
    pick_kv = jnp.where(have == target + 4, 1.0, 0.0).astype(BF16)

    def by_slot(k):
        return jnp.concatenate([att_buf[k % 2, 4 * g + k // 2] for g in range(16)], axis=0)

    for k in range(PREFILL_TP):
        picked = dot_n(pick_q, by_slot(k)).astype(BF16)
        for h in range(4):
            att[:, pl.ds((4 * k + h) * TILE, TILE)] = picked[32 * h : 32 * h + 32]
    copies[4].wait()
    mixed_part = dot_t(att[...], wo[...]).astype(BF16)
    shift = lax.rem(me * COLS, TILE)
    src_col = lax.broadcasted_iota(jnp.int32, (COLS, TILE), 0)
    dst_col = lax.broadcasted_iota(jnp.int32, (COLS, TILE), 1)
    put0 = jnp.where(dst_col == lax.rem(src_col + shift, TILE), 1.0, 0.0).astype(BF16)
    put1 = jnp.where(dst_col == lax.rem(src_col + shift + 64, TILE), 1.0, 0.0).astype(BF16)
    mix_buf[c, chip] = (dot_n(mixed_part[:16], put0) + dot_n(mixed_part[16:], put1)).astype(BF16)

    spread(mix_buf, 4)
    pages(2)
    for k in range(PREFILL_TP):
        picked = dot_n(pick_kv, by_slot(k)).astype(BF16)
        for a in range(2):
            nk_ref[:, pl.ds((2 * k + a) * TILE, TILE)] = picked[32 * a : 32 * a + 32]
            nv_ref[:, pl.ds((2 * k + a) * TILE, TILE)] = picked[64 + 32 * a : 96 + 32 * a]
    pages(3)
    take(mix_buf.at[0, pl.ds(0, CHIPS - 1)], rs.at[4])
    swap(mix_buf, 5)
    take(mix_buf.at[0], rs.at[5])

    lane16 = lax.broadcasted_iota(jnp.int32, (16, TILE), 1)

    def join(p, carry):
        straight, turned = [], []
        for i in range(32):
            piece = mix_buf[i % 2, p * 16 + i // 2].astype(F32)
            straight.append(piece)
            turned.append(pltpu.roll(piece, 64, 1))
        for t in range(9):
            top = bottom = None
            for i in range(32):
                lo, hi = COLS * i - TILE * t, COLS * i + COLS - TILE * t
                if hi <= 0 or lo >= TILE:
                    continue
                if top is None:
                    top, bottom = straight[i], turned[i]
                else:
                    later = lane16 >= lo
                    top = jnp.where(later, straight[i], top)
                    bottom = jnp.where(later, turned[i], bottom)
            column = pl.multiple_of((p * 9 + t) * TILE, TILE)
            mix[0:16, pl.ds(column, TILE)] = top
            mix[16:32, pl.ds(column, TILE)] = bottom
        return carry

    lax.fori_loop(0, 4, join, 0)
    stream[...] = hid[...] + rms_scale(mix[...], gain[1:2, :])
    ffn_in = rms_scale(stream[...], gain[2:3, :]).astype(BF16)
    copies[5].wait()
    gate = dot_t(ffn_in, wg[0])
    up = dot_t(ffn_in, wg[1])
    cube = gate + 0.044715 * (gate * gate * gate)
    active = (0.5 * gate * (1.0 + jnp.tanh(0.7978845608028654 * cube)) * up).astype(BF16)
    copies[6].wait()
    for n in range(4):
        columns = pl.ds(n * (D // 4), D // 4)
        piece = dot_n(active, wd[:, columns]).astype(BF16)
        br[0, :, columns] = piece[:16]
        br[1, :, columns] = piece[16:]

    send(br.at[1 - c], pr, 6, at(x, y, 1 - c))
    pages(4)
    take(pr, rs.at[6])
    sb[...] = (br[c].astype(F32) + pr[...].astype(F32)).astype(BF16)

    def send_sums(j, carry):
        owner = lax.div(j * 16, 9)
        tile = sb.at[:, pl.ds(pl.multiple_of(j * TILE, TILE), TILE)]

        @pl.when(owner != chip)
        def _():
            send(tile, rs_buf.at[chip], 7, at(lax.div(owner, NY), lax.rem(owner, NY), c))

        @pl.when(owner == chip)
        def _():
            rs_buf[chip] = tile[...]

        return carry

    lax.fori_loop(0, TILES, send_sums, 0)
    pages(5)
    my_tile = lax.div(chip * 9 + 15, 16)
    owns = lax.div(my_tile * 16, 9) == chip

    @pl.when(owns)
    def _():
        take(rs_buf.at[pl.ds(0, CHIPS - 1)], rs.at[7])
        total = jnp.zeros((16, TILE), F32)

        def add(i, acc):
            for n in range(8):
                acc = acc + rs_buf[i * 8 + n].astype(F32)
            return acc

        fin[c, my_tile] = lax.fori_loop(0, 8, add, total).astype(BF16)

        def tell(i, carry):
            tx = lax.rem(x + lax.div(i, NY), NX)
            ty = lax.rem(y + lax.rem(i, NY), NY)
            send(fin.at[c, my_tile], fin.at[c, my_tile], 8, at(tx, ty, c))
            return carry

        lax.fori_loop(1, CHIPS, tell, 0)

    pages(6)

    @pl.when(owns)
    def _():
        take(fin.at[0, pl.ds(0, TILES - 1)], rs.at[8])

    @pl.when(jnp.logical_not(owns))
    def _():
        take(fin.at[0, pl.ds(0, TILES)], rs.at[8])

    swap(fin, 9)
    pages(7)
    take(fin.at[0], rs.at[9])

    first = lax.div(me * COLS, TILE)
    second = jnp.minimum(first + 1, TILES - 1)
    for half in range(2):

        def square(j, acc):
            for n in range(4):
                tile = fin[half, j * 4 + n].astype(F32)
                acc = acc + tile * tile
            return acc

        squares = lax.fori_loop(0, TILES // 4, square, jnp.zeros((16, TILE), F32))
        factor = lax.rsqrt(jnp.sum(squares, axis=1, keepdims=True) / D + EPSILON)

        def block(t):
            columns = pl.ds(pl.multiple_of(t * TILE, TILE), TILE)
            branch = fin[half, t].astype(F32)
            value = stream[16 * half : 16 * half + 16, columns] + branch * factor * (1.0 + gain[3:4, columns])
            return pltpu.roll(value, lax.rem(TILE - shift, TILE), 1)

        res_ref[16 * half : 16 * half + 16, :] = jnp.where(lane16 < TILE - shift, block(first), block(second))

    own_copy.wait()
    take(arr.at[pl.ds(0, GROUP - 1)], rs.at[0])
    take(arr.at[pl.ds(0, GROUP - 1)], ss.at[0])

    @pl.when(keeps_one)
    def _():
        take(qr.at[pl.ds(0, 15)], ss.at[1])

    @pl.when(jnp.logical_not(keeps_one))
    def _():
        take(qr.at[pl.ds(0, 16)], ss.at[1])

    take(att_buf.at[0, pl.ds(0, CHIPS - 1)], ss.at[2])
    take(att_buf.at[0], ss.at[3])
    take(mix_buf.at[0, pl.ds(0, CHIPS - 1)], ss.at[4])
    take(mix_buf.at[0], ss.at[5])
    take(pr, ss.at[6])

    @pl.when(owns)
    def _():
        take(fin.at[0, pl.ds(0, TILES - 1)], ss.at[7])
        take(rs_buf.at[pl.ds(0, CHIPS - 1)], ss.at[8])

    @pl.when(jnp.logical_not(owns))
    def _():
        take(fin.at[0, pl.ds(0, TILES)], ss.at[7])

    take(fin.at[0], ss.at[9])


def on_device(
    hidden_in,
    prefill_cache,
    lengths,
    page_table,
    qkv_weight,
    out_weight,
    gate_up_weight,
    down_weight,
    norm_gains,
):
    me = lax.axis_index(TP)
    batch = hidden_in.shape[0]
    my_group = me // PREFILL_TP
    page_width = prefill_cache.shape[5]
    rows = lax.dynamic_slice_in_dim(page_table, my_group * 2, 2, 0)
    lens = lax.dynamic_slice_in_dim(lengths, my_group * 2, 2, 0)
    page_ids = jnp.arange(GROUP, dtype=jnp.int32)
    onehot = (rows[:, :, None] == page_ids[None, None, :]).astype(jnp.int32)
    inverse = jnp.sum(onehot * page_ids[None, :, None], axis=1)
    token = jnp.arange(page_width, dtype=jnp.int32)
    position = rows[:, :, None] * page_width + token[None, None, :]
    visible = (position < lens[:, None, None]).astype(F32).reshape(2, GROUP * page_width)
    half = HEAD_DIM // 2
    exponent = jnp.arange(half, dtype=F32) * (-2.0 / HEAD_DIM)
    angles = lens.astype(F32)[:, None] * jnp.power(jnp.float32(10000.0), exponent)
    cosine = jnp.cos(angles)
    sine = jnp.sin(angles)
    cos = jnp.concatenate([cosine, cosine], axis=1)
    sin = jnp.concatenate([-sine, sine], axis=1)
    paged = prefill_cache.reshape(2, 2, GROUP, page_width, 2 * HEAD_DIM)
    cache = prefill_cache.reshape(2, 2, GROUP * page_width, 2 * HEAD_DIM)
    k_cols = KV_HEADS * HEAD_DIM
    vmem = pl.BlockSpec(memory_space=pltpu.VMEM)
    hbm = pl.BlockSpec(memory_space=pl.ANY)
    dma = pltpu.SemaphoreType.DMA
    res, new_key, new_value, decoded = pl.pallas_call(
        step_kernel,
        name="step",
        out_shape=(
            jax.ShapeDtypeStruct((batch, TILE), F32),
            jax.ShapeDtypeStruct((batch, k_cols), BF16),
            jax.ShapeDtypeStruct((batch, k_cols), BF16),
            jax.ShapeDtypeStruct((1, 1, 2, batch, page_width, k_cols), BF16),
        ),
        in_specs=[pl.BlockSpec(memory_space=pltpu.SMEM)] + [vmem] * 3 + [hbm] * 8,
        out_specs=(vmem, vmem, vmem, hbm),
        scratch_shapes=[
            pltpu.VMEM((batch, D), F32),
            pltpu.VMEM(paged.shape, BF16),
            pltpu.VMEM(cache.shape, BF16),
            pltpu.VMEM(qkv_weight.shape[1:], BF16),
            pltpu.VMEM(out_weight.shape[1:], BF16),
            pltpu.VMEM(gate_up_weight.shape[1:], BF16),
            pltpu.VMEM(down_weight.shape[1:], BF16),
            pltpu.VMEM(norm_gains.shape[1:], F32),
            pltpu.VMEM((GROUP, 2, 2, page_width, 2 * HEAD_DIM), BF16),
            pltpu.VMEM((4, 8, TILE), F32),
            pltpu.VMEM((16, 8, TILE), F32),
            pltpu.VMEM((NC, CHIPS, 16, TILE), BF16),
            pltpu.VMEM((batch, HEADS * HEAD_DIM), BF16),
            pltpu.VMEM((NC, CHIPS, 16, TILE), BF16),
            pltpu.VMEM((batch, D), F32),
            pltpu.VMEM((batch, D), F32),
            pltpu.VMEM((2, 16, D), BF16),
            pltpu.VMEM((16, D), BF16),
            pltpu.VMEM((16, D), BF16),
            pltpu.VMEM((CHIPS, 16, TILE), BF16),
            pltpu.VMEM((NC, TILES, 16, TILE), BF16),
            dma((8,)),
            dma((1,)),
            dma((10,)),
            dma((10,)),
        ],
        compiler_params=pltpu.CompilerParams(
            collective_id=0, has_side_effects=True, vmem_limit_bytes=48 * 2**20
        ),
    )(inverse, visible, cos, sin, hidden_in, paged, cache, qkv_weight, out_weight, gate_up_weight, down_weight, norm_gains)
    my_pos = me * page_width + token
    fresh = (my_pos[None, :] == lengths[:, None])[None, None, None, :, :, None]
    new = jnp.stack([new_key, new_value], axis=0).reshape(1, 1, 2, batch, 1, k_cols)
    decode_cache = jnp.where(fresh, new, decoded)
    return (res[:, :COLS], decode_cache)


def solution(mesh):
    torus = Mesh(mesh.devices.reshape(mesh.shape["grp"], NX, NY, NC), ("grp",) + TP)
    return jax.shard_map(
        on_device,
        mesh=torus,
        in_specs=(
            P("grp", None),
            P(TP, None, None, "grp", None, None, None),
            P("grp"),
            P("grp", None),
            P(None, TP, None),
            P(None, TP, None),
            P(None, None, TP, None),
            P(None, TP, None),
            P(),
        ),
        out_specs=(P("grp", TP), P(TP, None, None, "grp", None, None)),
        check_vma=False,
    )
```

time: 439 us -> 124 us (0.28)
  blocking collectives: 264 us -> 0 us
  Pallas kernels: 0 us -> 112 us
  waiting for transfers between devices: 89.8 us -> 0 us
  local copies, waits for them, and re-layouts: 40.1 us -> 6.21 us
  between operations: 14.2 us -> 0.71 us
  other arithmetic: 17.5 us -> 4.26 us
  starting transfers between devices: 7.52 us -> 0 us
  matrix products: 5.66 us -> 0 us
    all_gather x5 -> x0, blocking collectives: 197 us -> none  [the longest x4 150 us: gather_in_order(): tiles = lax.all_gather(tiles, axes[k], axis=0, tiled=True)]
    pallas_call x0 -> x1, Pallas kernels: none -> 112 us  [on_device(): pl.pallas_call(step_kernel, name='step', out_shape=(jax.ShapeDtypeStruct(...]
    reduce_scatter x3 -> x0, waiting for transfers between devices: 89.6 us -> none  [own_block(): tiles = lax.psum_scatter(tiles, axes[k], scatter_dimension=0, tiled=True)]
    psum x3 -> x0, blocking collectives: 41.1 us -> none  [one_axis_at_a_time(): shard = lax.psum(shard, axis)]
    all_to_all x1 -> x0, blocking collectives: 25.5 us -> none  [turned_blocks(): lax.all_to_all(tiles, axes[k], split_axis=k, concat_axis=k, tiled=True)]
    reshape x7 -> x0, local copies, waits for them, and re-layouts: 11.9 us -> none  [the longest x1 3.33 us: on_device(): relaid.transpose(0, 1, 3, 2, 5, 4, 6, 7)]
    convert_element_type x3 -> x0, local copies, waits for them, and re-layouts: 7.39 us -> none  [the longest x2 6.21 us: on_device(): stream = stream + rms_scale(mixed_out.astype(jnp.float32), norm_gains[0, 1])]
    all_to_all x1 -> x0, starting transfers between devices: 7.33 us -> none  [turned_blocks(): lax.all_to_all(tiles, axes[k], split_axis=k, concat_axis=k, tiled=True)]
  transfers between devices with their start and end apart: 4 -> 0, of which waited for: 3 -> 0; matrix products, arithmetic and copies ran while one was open for 10% -> 0% of each run, Pallas kernels for 0% -> 0%
where the time goes in v1:
time: 124 us
  Pallas kernels  112 us (90%)
  local copies, waits for them, and re-layouts  6.21 us (5%)
  other arithmetic  4.26 us (3%)
    pallas_call x1, Pallas kernels, on_device(): pl.pallas_call(step_kernel, name='step', out_shape=(jax.ShapeDtypeStruct(...  112 us
    unnamed x11, local copies, waits for them, and re-layouts  5.91 us

profile of v1, /device:TPU:513, one launch (start us, length us, event | category | flops | bytes accessed | tf_op | source)
XLA Modules:
  0.0 123.6 jit_solution(9567379778214343894)
XLA Ops:
  0.7 0.7 fusion.1
  1.4 0.7 broadcast_multiply_fusion
  2.1 0.1 select_reduce_fusion.inv_ref
  2.2 0.1 fusion
  2.3 0.1 pad_maximum_fusion.1
  2.4 0.7 broadcast_compare_fusion
  3.2 0.1 add.47
  3.2 0.1 add.44
  3.3 0.1 add.45
  3.5 0.1 compare_convert_fusion.vis_ref
  3.5 0.0 copy-start
  3.5 1.3 %copy-done = bf16[1,144,4608]{2,1,0:T(8,128)(2,1)S(1)} copy-done((bf16[1,144,4608]{2,1,0:T(8,128)(2,1)S(1)}, bf16[1,144,4608]{2,1,0:T(8,128)(2,1)}, u32[]{:S(2)}) %copy-start) | copy-done | bytes 1327128
  4.9 0.0 copy-start.1
  4.9 1.1 copy-done.1
  5.9 0.0 copy-start.2
  5.9 1.1 copy-done.2
  7.0 0.0 copy-start.3
  7.0 1.0 copy-done.3
  8.0 0.0 copy-start.4
  8.0 0.9 copy-done.4
  8.8 112.5 %step.1 = (f32[32,128]{1,0:T(8,128)S(1)}, bf16[32,2048]{1,0:T(8,128)(2,1)S(1)}, bf16[32,2048]{1,0:T(8,128)(2,1)S(1)}, bf16[1,1,2,32,8,2048]{5,4,3,2,1,0:T(8,128)(2,1)S(1)}) custom-call(s32[2,128]{1,0:T(2,128)S(1)} %select_reduce_fusion.inv_ref, f32[2,1024]{1,0:T(2,128)S(1)} %compare_convert_fusion.vis_ref, f32[2,128]{1,0:T(2,128)S(1)} %get-tuple-element.17.cos_ref, ...), custom_call_target="tpu_custom_call" | custom-call | tf_op jit(solution)/shard_map/step/pallas_call | solution.py:447
  121.4 1.7 %broadcast_select_fusion = bf16[1,1,2,32,8,2048]{5,4,3,2,1,0:T(8,128)(2,1)} fusion(bf16[1,1,2,32,8,2048]{5,4,3,2,1,0:T(8,128)(2,1)S(1)} %get-tuple-element.9, pred[32,8]{1,0:T(8,128)(4,1)S(1)} %broadcast_compare_fusion, bf16[2,32,2048]{2,1,0:T(8,128)(2,1)S(1)} %pad_maximum_fusion), kind=kLoop, calls=%fused_computation | loop fusion | flops 1048576 | bytes 4456704 | tf_op jit(solution)/shard_map/jit(_where)/select_n | solution.py:492
  123.0 0.6 copy.12
  (4 shorter events, 0.0 us)
Async XLA Ops:
  3.5 1.3 %copy-start = (bf16[1,144,4608]{2,1,0:T(8,128)(2,1)S(1)}, bf16[1,144,4608]{2,1,0:T(8,128)(2,1)}, u32[]{:S(2)}) copy-start(bf16[1,144,4608]{2,1,0:T(8,128)(2,1)} %wd_hbm.1) | copy-start | bytes 3981316
  4.9 1.1 copy-start.1
  5.9 1.1 copy-start.2
  7.0 1.0 copy-start.3
  8.0 0.9 copy-start.4

commit v2 on v1

--- a/solution.py
+++ b/solution.py
@@ -1,5 +1,6 @@
 import jax
 import jax.numpy as jnp
+import numpy as np
 from jax import lax
 from jax.experimental import pallas as pl
 from jax.experimental.pallas import tpu as pltpu
@@ -25,7 +26,7 @@
 EPSILON = 1e-06
 SOFTCAP = 50.0
 
-A2A_POINTS = (16, 34, 50, 66, 84, 100, 116, 127)
+PAGES = (24, 24, 18, 12, 24, 25)
 
 
 def capped(raw_scores):
@@ -46,9 +47,9 @@
 
 
 def step_kernel(
-    inv_ref, vis_ref, cos_ref, sin_ref, hid_hbm, paged_hbm, cache_hbm, wq_hbm, wo_hbm, wg_hbm, wd_hbm, gain_hbm,
+    len_ref, table_hbm, freq_hbm, hid_hbm, paged_hbm, cache_hbm, wq_hbm, wo_hbm, wg_hbm, wd_hbm, gain_hbm,
     res_ref, nk_ref, nv_ref, dec_ref,
-    hid, paged, cache, wq, wo, wg, wd, gain, arr, qs, qr, att_buf, att, mix_buf, mix, stream,
+    table, freq, inv_v, inv, hid, paged, cache, wq, wo, wg, wd, gain, arr, qs, qr, att_buf, att, mix_buf, mix, stream,
     br, pr, sb, rs_buf, fin, in_sem, own_sem, ss, rs,
 ):
     grp = lax.axis_index("grp")
@@ -76,7 +77,8 @@
         return carry
 
     loads = [
-        (hid_hbm, hid), (gain_hbm.at[0], gain), (wq_hbm.at[0], wq), (paged_hbm, paged),
+        (table_hbm, table), (freq_hbm, freq), (hid_hbm, hid),
+        (gain_hbm.at[0], gain), (wq_hbm.at[0], wq), (paged_hbm, paged),
         (wo_hbm.at[0], wo), (wg_hbm.at[0], wg), (wd_hbm.at[0], wd), (cache_hbm, cache),
     ]
     copies = [pltpu.make_async_copy(s, d, in_sem.at[n]) for n, (s, d) in enumerate(loads)]
@@ -103,36 +105,68 @@
 
         lax.fori_loop(first, last, body, 0)
 
-    starts = (1,) + tuple(p + 1 for p in A2A_POINTS[:-1])
-    stops = tuple(p + 1 for p in A2A_POINTS)
-
     def pages(n):
-        send_pages(starts[n], stops[n])
+        first = 1 + sum(PAGES[:n])
+        send_pages(first, first + PAGES[n])
+
+    def other_chip(i):
+        n = i + lax.div(i, 36)
+        tx = lax.rem(x + 4 + lax.div(n, NY), NX)
+        ty = lax.rem(y + 4 + lax.rem(n, NY), NY)
+        return tx, ty
 
     def spread(buf, phase):
         def body(i, carry):
-            tx = lax.rem(x + lax.div(i, NY), NX)
-            ty = lax.rem(y + lax.rem(i, NY), NY)
+            tx, ty = other_chip(i)
             send(buf.at[c, chip], buf.at[c, chip], phase, at(tx, ty, c))
             return carry
 
-        lax.fori_loop(1, CHIPS, body, 0)
+        lax.fori_loop(0, CHIPS - 1, body, 0)
 
     def swap(buf, phase):
         send(buf.at[c], buf.at[c], phase, at(x, y, 1 - c))
 
-    copies[0].wait()
-    copies[1].wait()
+    copies[2].wait()
+    copies[3].wait()
     normed = rms_scale(hid[...], gain[0:1, :]).astype(BF16)
-    copies[2].wait()
+    copies[4].wait()
     part = dot_t(normed, wq[...]).astype(BF16).astype(F32)
     qs[...] = jnp.concatenate([part, part], axis=1).reshape(4, 8, TILE)
 
-    copies[3].wait()
+    copies[0].wait()
+    block = lax.broadcasted_iota(jnp.int32, (GROUP, GROUP), 0)
+    index = lax.broadcasted_iota(jnp.int32, (8, GROUP), 1).astype(F32).astype(BF16)
+    tables = []
+    for e in range(2):
+        row = table[pl.ds(my_group * 2 + e, 1), :]
+        tables.append(row)
+        hits = jnp.where(jnp.broadcast_to(row, (GROUP, GROUP)) == block, 1.0, 0.0).astype(BF16)
+        inv_v[8 * e : 8 * e + 8, :] = dot_t(index, hits).astype(jnp.int32)
+    to_scalars = pltpu.make_async_copy(inv_v, inv, own_sem.at[1])
+    to_scalars.start()
+
+    copies[1].wait()
+    slot_page = lax.broadcasted_iota(jnp.int32, (GROUP, GROUP * 8), 0)
+    slot_at = lax.broadcasted_iota(jnp.int32, (GROUP, GROUP * 8), 1)
+    widen = jnp.where(lax.div(slot_at, 8) == slot_page, 1.0, 0.0).astype(BF16)
+    token = lax.rem(lax.broadcasted_iota(jnp.int32, (8, GROUP * 8), 1), 8).astype(F32)
+    lane = lax.broadcasted_iota(jnp.int32, (8, TILE), 1)
+    seen, cosines, sines = [], [], []
+    for e in range(2):
+        length = len_ref[my_group * 2 + e].astype(F32)
+        row = jnp.broadcast_to(tables[e], (8, GROUP)).astype(F32).astype(BF16)
+        seen.append(dot_n(row, widen) * 8.0 + token < length)
+        angle = jnp.broadcast_to(freq[...], (8, TILE)) * length
+        sine = jnp.sin(angle)
+        cosines.append(jnp.cos(angle))
+        sines.append(jnp.where(lane < HEAD_DIM // 2, -sine, sine))
+
+    copies[5].wait()
+    to_scalars.wait()
 
     def arrange(q, carry):
         for e in range(2):
-            page = inv_ref[e, q]
+            page = jnp.maximum(jnp.minimum(inv[8 * e, q], GROUP - 1), 0)
             for kv in range(2):
                 arr[q, kv, e] = paged[kv, e, page]
         return carry
@@ -177,17 +211,15 @@
     def _():
         take(qr.at[pl.ds(0, 16)], rs.at[1])
 
-    copies[7].wait()
-
-    lane = lax.broadcasted_iota(jnp.int32, (8, TILE), 1)
+    copies[9].wait()
+
     rows8 = lax.broadcasted_iota(jnp.int32, (8, TILE), 0)
     rows16 = lax.broadcasted_iota(jnp.int32, (16, TILE), 0)
     scale = (D / HEADS) ** (-0.5)
     message = jnp.zeros((16, TILE), F32)
     row0 = lax.rem(my_group, 4) * 2
     for e in range(2):
-        cos = jnp.broadcast_to(cos_ref[e : e + 1, :], (8, TILE))
-        sin = jnp.broadcast_to(sin_ref[e : e + 1, :], (8, TILE))
+        cos, sin = cosines[e], sines[e]
 
         def head(i):
             low = jnp.broadcast_to(qr[2 * i, pl.ds(row0 + e, 1), :], (8, TILE))
@@ -207,8 +239,7 @@
         own = jnp.exp(capped(own_raw))
         both = jnp.concatenate([left, right], axis=1).astype(BF16)
         raw = dot_t(both, cache[0, e]) * scale
-        seen = jnp.broadcast_to(vis_ref[e : e + 1, :], raw.shape)
-        weights = jnp.where(seen > 0.5, jnp.exp(capped(raw)), 0.0)
+        weights = jnp.where(seen[e], jnp.exp(capped(raw)), 0.0)
         den = jnp.sum(weights, axis=1, keepdims=True) + own
         num = dot_n(weights.astype(BF16), cache[1, e])
         own_b = own.astype(BF16).astype(F32)
@@ -238,7 +269,7 @@
         picked = dot_n(pick_q, by_slot(k)).astype(BF16)
         for h in range(4):
             att[:, pl.ds((4 * k + h) * TILE, TILE)] = picked[32 * h : 32 * h + 32]
-    copies[4].wait()
+    copies[6].wait()
     mixed_part = dot_t(att[...], wo[...]).astype(BF16)
     shift = lax.rem(me * COLS, TILE)
     src_col = lax.broadcasted_iota(jnp.int32, (COLS, TILE), 0)
@@ -287,12 +318,12 @@
     lax.fori_loop(0, 4, join, 0)
     stream[...] = hid[...] + rms_scale(mix[...], gain[1:2, :])
     ffn_in = rms_scale(stream[...], gain[2:3, :]).astype(BF16)
-    copies[5].wait()
+    copies[7].wait()
     gate = dot_t(ffn_in, wg[0])
     up = dot_t(ffn_in, wg[1])
     cube = gate + 0.044715 * (gate * gate * gate)
     active = (0.5 * gate * (1.0 + jnp.tanh(0.7978845608028654 * cube)) * up).astype(BF16)
-    copies[6].wait()
+    copies[8].wait()
     for n in range(4):
         columns = pl.ds(n * (D // 4), D // 4)
         piece = dot_n(active, wd[:, columns]).astype(BF16)
@@ -300,7 +331,6 @@
         br[1, :, columns] = piece[16:]
 
     send(br.at[1 - c], pr, 6, at(x, y, 1 - c))
-    pages(4)
     take(pr, rs.at[6])
     sb[...] = (br[c].astype(F32) + pr[...].astype(F32)).astype(BF16)
 
@@ -319,7 +349,7 @@
         return carry
 
     lax.fori_loop(0, TILES, send_sums, 0)
-    pages(5)
+    pages(4)
     my_tile = lax.div(chip * 9 + 15, 16)
     owns = lax.div(my_tile * 16, 9) == chip
 
@@ -336,14 +366,13 @@
         fin[c, my_tile] = lax.fori_loop(0, 8, add, total).astype(BF16)
 
         def tell(i, carry):
-            tx = lax.rem(x + lax.div(i, NY), NX)
-            ty = lax.rem(y + lax.rem(i, NY), NY)
+            tx, ty = other_chip(i)
             send(fin.at[c, my_tile], fin.at[c, my_tile], 8, at(tx, ty, c))
             return carry
 
-        lax.fori_loop(1, CHIPS, tell, 0)
-
-    pages(6)
+        lax.fori_loop(0, CHIPS - 1, tell, 0)
+
+    pages(5)
 
     @pl.when(owns)
     def _():
@@ -354,7 +383,6 @@
         take(fin.at[0, pl.ds(0, TILES)], rs.at[8])
 
     swap(fin, 9)
-    pages(7)
     take(fin.at[0], rs.at[9])
 
     first = lax.div(me * COLS, TILE)
@@ -421,28 +449,15 @@
 ):
     me = lax.axis_index(TP)
     batch = hidden_in.shape[0]
-    my_group = me // PREFILL_TP
     page_width = prefill_cache.shape[5]
-    rows = lax.dynamic_slice_in_dim(page_table, my_group * 2, 2, 0)
-    lens = lax.dynamic_slice_in_dim(lengths, my_group * 2, 2, 0)
-    page_ids = jnp.arange(GROUP, dtype=jnp.int32)
-    onehot = (rows[:, :, None] == page_ids[None, None, :]).astype(jnp.int32)
-    inverse = jnp.sum(onehot * page_ids[None, :, None], axis=1)
-    token = jnp.arange(page_width, dtype=jnp.int32)
-    position = rows[:, :, None] * page_width + token[None, None, :]
-    visible = (position < lens[:, None, None]).astype(F32).reshape(2, GROUP * page_width)
-    half = HEAD_DIM // 2
-    exponent = jnp.arange(half, dtype=F32) * (-2.0 / HEAD_DIM)
-    angles = lens.astype(F32)[:, None] * jnp.power(jnp.float32(10000.0), exponent)
-    cosine = jnp.cos(angles)
-    sine = jnp.sin(angles)
-    cos = jnp.concatenate([cosine, cosine], axis=1)
-    sin = jnp.concatenate([-sine, sine], axis=1)
+    exponent = np.arange(HEAD_DIM // 2, dtype=np.float32) * np.float32(-2.0 / HEAD_DIM)
+    frequency = np.power(np.float32(10000.0), exponent).astype(np.float32)
+    frequency = jnp.asarray(np.concatenate([frequency, frequency])[None, :])
     paged = prefill_cache.reshape(2, 2, GROUP, page_width, 2 * HEAD_DIM)
     cache = prefill_cache.reshape(2, 2, GROUP * page_width, 2 * HEAD_DIM)
     k_cols = KV_HEADS * HEAD_DIM
     vmem = pl.BlockSpec(memory_space=pltpu.VMEM)
-    hbm = pl.BlockSpec(memory_space=pl.ANY)
+    hbm = pl.BlockSpec(memory_space=pltpu.HBM)
     dma = pltpu.SemaphoreType.DMA
     res, new_key, new_value, decoded = pl.pallas_call(
         step_kernel,
@@ -453,9 +468,13 @@
             jax.ShapeDtypeStruct((batch, k_cols), BF16),
             jax.ShapeDtypeStruct((1, 1, 2, batch, page_width, k_cols), BF16),
         ),
-        in_specs=[pl.BlockSpec(memory_space=pltpu.SMEM)] + [vmem] * 3 + [hbm] * 8,
-        out_specs=(vmem, vmem, vmem, hbm),
+        in_specs=[pl.BlockSpec(memory_space=pltpu.SMEM)] + [hbm] * 10,
+        out_specs=(vmem, vmem, vmem, pl.BlockSpec(memory_space=pl.ANY)),
         scratch_shapes=[
+            pltpu.VMEM(page_table.shape, jnp.int32),
+            pltpu.VMEM(frequency.shape, F32),
+            pltpu.VMEM((16, GROUP), jnp.int32),
+            pltpu.SMEM((16, GROUP), jnp.int32),
             pltpu.VMEM((batch, D), F32),
             pltpu.VMEM(paged.shape, BF16),
             pltpu.VMEM(cache.shape, BF16),
@@ -477,16 +496,16 @@
             pltpu.VMEM((16, D), BF16),
             pltpu.VMEM((CHIPS, 16, TILE), BF16),
             pltpu.VMEM((NC, TILES, 16, TILE), BF16),
-            dma((8,)),
-            dma((1,)),
+            dma((10,)),
+            dma((2,)),
             dma((10,)),
             dma((10,)),
         ],
         compiler_params=pltpu.CompilerParams(
-            collective_id=0, has_side_effects=True, vmem_limit_bytes=48 * 2**20
+            collective_id=0, has_side_effects=True, vmem_limit_bytes=67043328
         ),
-    )(inverse, visible, cos, sin, hidden_in, paged, cache, qkv_weight, out_weight, gate_up_weight, down_weight, norm_gains)
-    my_pos = me * page_width + token
+    )(lengths, page_table, frequency, hidden_in, paged, cache, qkv_weight, out_weight, gate_up_weight, down_weight, norm_gains)
+    my_pos = me * page_width + jnp.arange(page_width, dtype=jnp.int32)
     fresh = (my_pos[None, :] == lengths[:, None])[None, None, None, :, :, None]
     new = jnp.stack([new_key, new_value], axis=0).reshape(1, 1, 2, batch, 1, k_cols)
     decode_cache = jnp.where(fresh, new, decoded)

time: 124 us -> 114 us (0.919)
  local copies, waits for them, and re-layouts: 6.21 us -> 0.61 us
  Pallas kernels: 112 us -> 107 us
  other arithmetic: 4.26 us -> 5.57 us
    pallas_call x1, Pallas kernels: 112 us -> 107 us  [on_device(): pl.pallas_call(step_kernel, name='step', out_shape=(jax.ShapeDtypeStruct(...]
    unnamed x11 -> x3, local copies, waits for them, and re-layouts: 5.91 us -> 0.61 us
    select_n x1, other arithmetic: 1.68 us -> 3.25 us  [on_device(): decode_cache = jnp.where(fresh, new, decoded)]
where the time goes in v2:
time: 114 us
  Pallas kernels  107 us (94%)
  other arithmetic  5.57 us (5%)
    pallas_call x1, Pallas kernels, on_device(): pl.pallas_call(step_kernel, name='step', out_shape=(jax.ShapeDtypeStruct(...  107 us
    select_n x1, other arithmetic, on_device(): decode_cache = jnp.where(fresh, new, decoded)  3.25 us

profile of v2, /device:TPU:513, one launch (start us, length us, event | category | flops | bytes accessed | tf_op | source)
XLA Modules:
  0.0 113.9 jit_solution(1261717461817346515)
XLA Ops:
  0.6 1.3 %broadcast_compare_fusion = pred[32,8]{1,0:T(8,128)(4,1)} fusion(s32[8]{0:T(128)S(1)} %iota_add_fusion, s32[32]{0:T(128)} %len_ref.1), kind=kLoop, calls=%fused_computation.2 | loop fusion | flops 256 | bytes 416 | tf_op jit(solution)/shard_map/eq | solution.py:509
  2.0 107.1 %step.1 = (f32[32,128]{1,0:T(8,128)}, bf16[32,2048]{1,0:T(8,128)(2,1)}, bf16[32,2048]{1,0:T(8,128)(2,1)}, bf16[1,1,2,32,8,2048]{5,4,3,2,1,0:T(8,128)(2,1)}) custom-call(s32[32]{0:T(128)} %len_ref.1, s32[32,128]{1,0:T(8,128)} %table_hbm.1, f32[1,128]{1,0:T(1,128)} %constant.20.clone.freq_hbm, f32[32,4608]{1,0:T(8,128)} %hid_hbm.1, ...), custom_call_target="tpu_custom_call" | custom-call | tf_op jit(solution)/shard_map/step/pallas_call | solution.py:462
  109.0 1.0 pad_maximum_fusion
  110.0 0.0 copy-start
  110.1 3.2 %broadcast_select_fusion = bf16[1,1,2,32,8,2048]{5,4,3,2,1,0:T(8,128)(2,1)} fusion(bf16[1,1,2,32,8,2048]{5,4,3,2,1,0:T(8,128)(2,1)} %get-tuple-element.9, pred[32,8]{1,0:T(8,128)(4,1)} %broadcast_compare_fusion, bf16[2,32,2048]{2,1,0:T(8,128)(2,1)S(1)} %pad_maximum_fusion), kind=kLoop, calls=%fused_computation | loop fusion | flops 1048576 | bytes 4456704 | tf_op jit(solution)/shard_map/jit(_where)/select_n | solution.py:511
  113.3 0.0 copy-done
  113.3 0.6 copy.13
  (1 shorter events, 0.0 us)
Async XLA Ops:
  110.0 3.3 %copy-start = (f32[32,128]{1,0:T(8,128)S(1)}, f32[32,128]{1,0:T(8,128)}, u32[]{:S(2)}) copy-start(f32[32,128]{1,0:T(8,128)} %get-tuple-element.6) | copy-start | bytes 49156

commit v3 on v2

--- a/solution.py
+++ b/solution.py
@@ -26,7 +26,7 @@
 EPSILON = 1e-06
 SOFTCAP = 50.0
 
-PAGES = (24, 24, 18, 12, 24, 25)
+PAGES = (24, 12, 18, 12, 18, 20, 23)
 
 
 def capped(raw_scores):
@@ -49,7 +49,7 @@
 def step_kernel(
     len_ref, table_hbm, freq_hbm, hid_hbm, paged_hbm, cache_hbm, wq_hbm, wo_hbm, wg_hbm, wd_hbm, gain_hbm,
     res_ref, nk_ref, nv_ref, dec_ref,
-    table, freq, inv_v, inv, hid, paged, cache, wq, wo, wg, wd, gain, arr, qs, qr, att_buf, att, mix_buf, mix, stream,
+    table, freq, inv_v, inv, hid, paged, cache, wq, wo, wg, wd, gain, arr, qs, qr, qf, att_buf, att, mix_buf, mix, stream,
     br, pr, sb, rs_buf, fin, in_sem, own_sem, ss, rs,
 ):
     grp = lax.axis_index("grp")
@@ -115,13 +115,34 @@
         ty = lax.rem(y + 4 + lax.rem(n, NY), NY)
         return tx, ty
 
-    def spread(buf, phase):
-        def body(i, carry):
-            tx, ty = other_chip(i)
-            send(buf.at[c, chip], buf.at[c, chip], phase, at(tx, ty, c))
-            return carry
-
-        lax.fori_loop(0, CHIPS - 1, body, 0)
+    x2, xp, y2, yp = lax.div(x, 2), lax.rem(x, 2), lax.div(y, 2), lax.rem(y, 2)
+    even = 1 - lax.rem(x + y, 2)
+
+    def mine(buf):
+        return buf.at[c, x2, xp, y2, yp]
+
+    def first_leg(buf, phase):
+        for o in (4, 3, 5, 2, 6, 1, 7):
+            target = at(lax.rem(x + even * o, NX), lax.rem(y + (1 - even) * o, NY), c)
+            send(mine(buf), mine(buf), phase, target)
+
+    def second_leg(buf, phase):
+        take(rs_buf.at[pl.ds(0, 7)], rs.at[phase])
+        row = buf.at[c, :, yp, y2, yp]
+        column = buf.at[c, x2, xp, :, 1 - xp]
+        for o in (4, 3, 5, 2, 6, 1, 7):
+            send(row, row, phase + 1, at(x, lax.rem(y + o, NY), c))
+            send(column, column, phase + 1, at(lax.rem(x + o, NX), y, c))
+
+    def last_leg(buf, phase):
+        take(rs_buf.at[pl.ds(0, 56)], rs.at[phase + 1])
+        swap(buf, phase + 2)
+        take(buf.at[0], rs.at[phase + 2])
+
+    def gone(buf, phase):
+        take(rs_buf.at[pl.ds(0, 7)], ss.at[phase])
+        take(rs_buf.at[pl.ds(0, 56)], ss.at[phase + 1])
+        take(buf.at[0], ss.at[phase + 2])
 
     def swap(buf, phase):
         send(buf.at[c], buf.at[c], phase, at(x, y, 1 - c))
@@ -130,8 +151,10 @@
     copies[3].wait()
     normed = rms_scale(hid[...], gain[0:1, :]).astype(BF16)
     copies[4].wait()
-    part = dot_t(normed, wq[...]).astype(BF16).astype(F32)
-    qs[...] = jnp.concatenate([part, part], axis=1).reshape(4, 8, TILE)
+    part = dot_t(normed, wq[...]).astype(BF16)
+    part = jnp.concatenate([part, part], axis=1)
+    for t in range(4):
+        qs[t] = part[8 * t : 8 * t + 8]
 
     copies[0].wait()
     block = lax.broadcasted_iota(jnp.int32, (GROUP, GROUP), 0)
@@ -185,13 +208,13 @@
     def send_heads(i, carry):
         tx = lax.rem(x + lax.div(i, 2), NX)
         ty = ty4 + 4 * lax.rem(i, 2)
-        mine = (tx == x) & (ty == y) & (tc4 == c)
-
-        @pl.when(jnp.logical_not(mine))
+        same = (tx == x) & (ty == y) & (tc4 == c)
+
+        @pl.when(jnp.logical_not(same))
         def _():
             send(qs.at[lax.div(tx, 2)], qr.at[slot], 1, at(tx, ty, tc4))
 
-        @pl.when(mine)
+        @pl.when(same)
         def _():
             qr[slot] = qs[lax.div(tx, 2)]
 
@@ -212,6 +235,8 @@
         take(qr.at[pl.ds(0, 16)], rs.at[1])
 
     copies[9].wait()
+
+    qf[...] = qr[...].astype(F32)
 
     rows8 = lax.broadcasted_iota(jnp.int32, (8, TILE), 0)
     rows16 = lax.broadcasted_iota(jnp.int32, (16, TILE), 0)
@@ -222,8 +247,8 @@
         cos, sin = cosines[e], sines[e]
 
         def head(i):
-            low = jnp.broadcast_to(qr[2 * i, pl.ds(row0 + e, 1), :], (8, TILE))
-            high = jnp.broadcast_to(qr[2 * i + 1, pl.ds(row0 + e, 1), :], (8, TILE))
+            low = jnp.broadcast_to(qf[2 * i, pl.ds(row0 + e, 1), :], (8, TILE))
+            high = jnp.broadcast_to(qf[2 * i + 1, pl.ds(row0 + e, 1), :], (8, TILE))
             return jnp.where(lane < HEAD_DIM // 2, low, high)
 
         def turned(u):
@@ -248,13 +273,13 @@
         rows = [out_l[0:1], out_l[1:2], out_r[2:3], out_r[3:4], k[0][0:1], k[1][0:1], v[0][0:1], v[1][0:1]]
         for j, row in enumerate(rows):
             message = jnp.where(rows16 == e * 8 + j, jnp.broadcast_to(row, (16, TILE)), message)
-    att_buf[c, chip] = message.astype(BF16)
-
-    spread(att_buf, 2)
+    att_buf[c, x2, xp, y2, yp] = message.astype(BF16)
+
+    first_leg(att_buf, 2)
     pages(1)
-    take(att_buf.at[0, pl.ds(0, CHIPS - 1)], rs.at[2])
-    swap(att_buf, 3)
-    take(att_buf.at[0], rs.at[3])
+    second_leg(att_buf, 2)
+    pages(2)
+    last_leg(att_buf, 2)
 
     want = lax.broadcasted_iota(jnp.int32, (128, 256), 0)
     have = lax.broadcasted_iota(jnp.int32, (128, 256), 1)
@@ -263,7 +288,11 @@
     pick_kv = jnp.where(have == target + 4, 1.0, 0.0).astype(BF16)
 
     def by_slot(k):
-        return jnp.concatenate([att_buf[k % 2, 4 * g + k // 2] for g in range(16)], axis=0)
+        blocks = []
+        for g in range(16):
+            ay = (g % 2) * 4 + k // 2
+            blocks.append(att_buf[k % 2, g // 4, (g // 2) % 2, ay // 2, ay % 2])
+        return jnp.concatenate(blocks, axis=0)
 
     for k in range(PREFILL_TP):
         picked = dot_n(pick_q, by_slot(k)).astype(BF16)
@@ -276,26 +305,25 @@
     dst_col = lax.broadcasted_iota(jnp.int32, (COLS, TILE), 1)
     put0 = jnp.where(dst_col == lax.rem(src_col + shift, TILE), 1.0, 0.0).astype(BF16)
     put1 = jnp.where(dst_col == lax.rem(src_col + shift + 64, TILE), 1.0, 0.0).astype(BF16)
-    mix_buf[c, chip] = (dot_n(mixed_part[:16], put0) + dot_n(mixed_part[16:], put1)).astype(BF16)
-
-    spread(mix_buf, 4)
-    pages(2)
+    mix_buf[c, x2, xp, y2, yp] = (dot_n(mixed_part[:16], put0) + dot_n(mixed_part[16:], put1)).astype(BF16)
+
+    first_leg(mix_buf, 5)
+    pages(3)
     for k in range(PREFILL_TP):
         picked = dot_n(pick_kv, by_slot(k)).astype(BF16)
         for a in range(2):
             nk_ref[:, pl.ds((2 * k + a) * TILE, TILE)] = picked[32 * a : 32 * a + 32]
             nv_ref[:, pl.ds((2 * k + a) * TILE, TILE)] = picked[64 + 32 * a : 96 + 32 * a]
-    pages(3)
-    take(mix_buf.at[0, pl.ds(0, CHIPS - 1)], rs.at[4])
-    swap(mix_buf, 5)
-    take(mix_buf.at[0], rs.at[5])
+    second_leg(mix_buf, 5)
+    pages(4)
+    last_leg(mix_buf, 5)
 
     lane16 = lax.broadcasted_iota(jnp.int32, (16, TILE), 1)
 
     def join(p, carry):
         straight, turned = [], []
         for i in range(32):
-            piece = mix_buf[i % 2, p * 16 + i // 2].astype(F32)
+            piece = mix_buf[i % 2, p, i // 16, (i % 16) // 4, (i // 2) % 2].astype(F32)
             straight.append(piece)
             turned.append(pltpu.roll(piece, 64, 1))
         for t in range(9):
@@ -330,8 +358,8 @@
         br[0, :, columns] = piece[:16]
         br[1, :, columns] = piece[16:]
 
-    send(br.at[1 - c], pr, 6, at(x, y, 1 - c))
-    take(pr, rs.at[6])
+    send(br.at[1 - c], pr, 8, at(x, y, 1 - c))
+    take(pr, rs.at[8])
     sb[...] = (br[c].astype(F32) + pr[...].astype(F32)).astype(BF16)
 
     def send_sums(j, carry):
@@ -340,7 +368,7 @@
 
         @pl.when(owner != chip)
         def _():
-            send(tile, rs_buf.at[chip], 7, at(lax.div(owner, NY), lax.rem(owner, NY), c))
+            send(tile, rs_buf.at[chip], 9, at(lax.div(owner, NY), lax.rem(owner, NY), c))
 
         @pl.when(owner == chip)
         def _():
@@ -349,13 +377,13 @@
         return carry
 
     lax.fori_loop(0, TILES, send_sums, 0)
-    pages(4)
+    pages(5)
     my_tile = lax.div(chip * 9 + 15, 16)
     owns = lax.div(my_tile * 16, 9) == chip
 
     @pl.when(owns)
     def _():
-        take(rs_buf.at[pl.ds(0, CHIPS - 1)], rs.at[7])
+        take(rs_buf.at[pl.ds(0, CHIPS - 1)], rs.at[9])
         total = jnp.zeros((16, TILE), F32)
 
         def add(i, acc):
@@ -367,23 +395,23 @@
 
         def tell(i, carry):
             tx, ty = other_chip(i)
-            send(fin.at[c, my_tile], fin.at[c, my_tile], 8, at(tx, ty, c))
+            send(fin.at[c, my_tile], fin.at[c, my_tile], 10, at(tx, ty, c))
             return carry
 
         lax.fori_loop(0, CHIPS - 1, tell, 0)
 
-    pages(5)
+    pages(6)
 
     @pl.when(owns)
     def _():
-        take(fin.at[0, pl.ds(0, TILES - 1)], rs.at[8])
+        take(fin.at[0, pl.ds(0, TILES - 1)], rs.at[10])
 
     @pl.when(jnp.logical_not(owns))
     def _():
-        take(fin.at[0, pl.ds(0, TILES)], rs.at[8])
-
-    swap(fin, 9)
-    take(fin.at[0], rs.at[9])
+        take(fin.at[0, pl.ds(0, TILES)], rs.at[10])
+
+    swap(fin, 11)
+    take(fin.at[0], rs.at[11])
 
     first = lax.div(me * COLS, TILE)
     second = jnp.minimum(first + 1, TILES - 1)
@@ -418,22 +446,20 @@
     def _():
         take(qr.at[pl.ds(0, 16)], ss.at[1])
 
-    take(att_buf.at[0, pl.ds(0, CHIPS - 1)], ss.at[2])
-    take(att_buf.at[0], ss.at[3])
-    take(mix_buf.at[0, pl.ds(0, CHIPS - 1)], ss.at[4])
-    take(mix_buf.at[0], ss.at[5])
-    take(pr, ss.at[6])
+    gone(att_buf, 2)
+    gone(mix_buf, 5)
+    take(pr, ss.at[8])
 
     @pl.when(owns)
     def _():
-        take(fin.at[0, pl.ds(0, TILES - 1)], ss.at[7])
-        take(rs_buf.at[pl.ds(0, CHIPS - 1)], ss.at[8])
+        take(fin.at[0, pl.ds(0, TILES - 1)], ss.at[9])
+        take(rs_buf.at[pl.ds(0, CHIPS - 1)], ss.at[10])
 
     @pl.when(jnp.logical_not(owns))
     def _():
-        take(fin.at[0, pl.ds(0, TILES)], ss.at[7])
-
-    take(fin.at[0], ss.at[9])
+        take(fin.at[0, pl.ds(0, TILES)], ss.at[9])
+
+    take(fin.at[0], ss.at[11])
 
 
 def on_device(
@@ -484,11 +510,12 @@
             pltpu.VMEM(down_weight.shape[1:], BF16),
             pltpu.VMEM(norm_gains.shape[1:], F32),
             pltpu.VMEM((GROUP, 2, 2, page_width, 2 * HEAD_DIM), BF16),
-            pltpu.VMEM((4, 8, TILE), F32),
+            pltpu.VMEM((4, 8, TILE), BF16),
+            pltpu.VMEM((16, 8, TILE), BF16),
             pltpu.VMEM((16, 8, TILE), F32),
-            pltpu.VMEM((NC, CHIPS, 16, TILE), BF16),
+            pltpu.VMEM((NC, NX // 2, 2, NY // 2, 2, 16, TILE), BF16),
             pltpu.VMEM((batch, HEADS * HEAD_DIM), BF16),
-            pltpu.VMEM((NC, CHIPS, 16, TILE), BF16),
+            pltpu.VMEM((NC, NX // 2, 2, NY // 2, 2, 16, TILE), BF16),
             pltpu.VMEM((batch, D), F32),
             pltpu.VMEM((batch, D), F32),
             pltpu.VMEM((2, 16, D), BF16),
@@ -498,13 +525,21 @@
             pltpu.VMEM((NC, TILES, 16, TILE), BF16),
             dma((10,)),
             dma((2,)),
-            dma((10,)),
-            dma((10,)),
+            dma((12,)),
+            dma((12,)),
         ],
         compiler_params=pltpu.CompilerParams(
-            collective_id=0, has_side_effects=True, vmem_limit_bytes=67043328
+            collective_id=0, has_side_effects=True, vmem_limit_bytes=48 * 2**20
         ),
-    )(lengths, page_table, frequency, hidden_in, paged, cache, qkv_weight, out_weight, gate_up_weight, down_weight, norm_gains)
+    )(
+        *[
+            pltpu.with_memory_space_constraint(operand, pltpu.HBM)
+            for operand in (
+                lengths, page_table, frequency, hidden_in, paged, cache,
+                qkv_weight, out_weight, gate_up_weight, down_weight, norm_gains,
+            )
+        ]
+    )
     my_pos = me * page_width + jnp.arange(page_width, dtype=jnp.int32)
     fresh = (my_pos[None, :] == lengths[:, None])[None, None, None, :, :, None]
     new = jnp.stack([new_key, new_value], axis=0).reshape(1, 1, 2, batch, 1, k_cols)

time: 114 us -> 107 us (0.939)
  Pallas kernels: 107 us -> 103 us
  other arithmetic: 5.57 us -> 2.41 us
    pallas_call x1, Pallas kernels: 107 us -> 103 us  [on_device(): pl.pallas_call(step_kernel, name='step', out_shape=(jax.ShapeDtypeStruct(...]
    select_n x1, other arithmetic: 3.25 us -> 1.65 us  [on_device(): decode_cache = jnp.where(fresh, new, decoded)]
where the time goes in v3:
time: 107 us
  Pallas kernels  103 us (96%)
  other arithmetic  2.41 us (2%)
    pallas_call x1, Pallas kernels, on_device(): pl.pallas_call(step_kernel, name='step', out_shape=(jax.ShapeDtypeStruct(...  103 us

profile of v3, /device:TPU:513, one launch (start us, length us, event | category | flops | bytes accessed | tf_op | source)
XLA Modules:
  0.0 106.9 jit_solution(1615780612445178282)
XLA Ops:
  0.6 0.7 broadcast_compare_fusion
  1.4 103.2 %step.1 = (f32[32,128]{1,0:T(8,128)S(1)}, bf16[32,2048]{1,0:T(8,128)(2,1)S(1)}, bf16[32,2048]{1,0:T(8,128)(2,1)S(1)}, bf16[1,1,2,32,8,2048]{5,4,3,2,1,0:T(8,128)(2,1)S(1)}) custom-call(s32[32]{0:T(128)} %len_ref.1, s32[32,128]{1,0:T(8,128)} %table_hbm.1, f32[1,128]{1,0:T(1,128)} %constant.20.clone.freq_hbm, f32[32,4608]{1,0:T(8,128)} %hid_hbm.1, ...), custom_call_target="tpu_custom_call" | custom-call | tf_op jit(solution)/shard_map/step/pallas_call | solution.py:488
  104.6 1.6 %broadcast_select_fusion = bf16[1,1,2,32,8,2048]{5,4,3,2,1,0:T(8,128)(2,1)} fusion(bf16[1,1,2,32,8,2048]{5,4,3,2,1,0:T(8,128)(2,1)S(1)} %get-tuple-element.9, pred[32,8]{1,0:T(8,128)(4,1)S(1)} %broadcast_compare_fusion, bf16[2,32,2048]{2,1,0:T(8,128)(2,1)S(1)} %pad_maximum_fusion), kind=kLoop, calls=%fused_computation | loop fusion | flops 1048576 | bytes 4456704 | tf_op jit(solution)/shard_map/jit(_where)/select_n | solution.py:546
  106.3 0.6 copy.13
  (2 shorter events, 0.0 us)

commit v4 on v3

--- a/solution.py
+++ b/solution.py
@@ -26,7 +26,7 @@
 EPSILON = 1e-06
 SOFTCAP = 50.0
 
-PAGES = (24, 12, 18, 12, 18, 20, 23)
+PAGES = (24, 12, 18, 0, 12, 18, 0, 20, 23)
 
 
 def capped(raw_scores):
@@ -50,7 +50,7 @@
     len_ref, table_hbm, freq_hbm, hid_hbm, paged_hbm, cache_hbm, wq_hbm, wo_hbm, wg_hbm, wd_hbm, gain_hbm,
     res_ref, nk_ref, nv_ref, dec_ref,
     table, freq, inv_v, inv, hid, paged, cache, wq, wo, wg, wd, gain, arr, qs, qr, qf, att_buf, att, mix_buf, mix, stream,
-    br, pr, sb, rs_buf, fin, in_sem, own_sem, ss, rs,
+    br, pr, sb, rs_buf, fin, sqs, marks, in_sem, own_sem, ss, rs,
 ):
     grp = lax.axis_index("grp")
     x = lax.axis_index("tp_0")
@@ -95,19 +95,39 @@
     def take(ref, sem):
         pltpu.make_async_copy(ref, ref, sem).wait()
 
+    def each(first, last, width, body):
+        whole = (last - first) // width
+
+        def several(n, carry):
+            for k in range(width):
+                body(first + n * width + k)
+            return carry
+
+        if whole:
+            lax.fori_loop(0, whole, several, 0)
+        for n in range(first + whole * width, last):
+            body(n)
+
     dec_mine = dec_ref.at[0, 0, :, pl.ds(my_group * 2, 2), :, pl.ds(pl.multiple_of(my_slot * 256, 256), 256)]
 
-    def send_pages(first, last):
-        def body(j, carry):
-            tx, ty, tc = peer(lax.rem(j * 37, GROUP))
-            send(arr.at[(tx * NY + ty) * NC + tc], dec_mine, 0, at(tx, ty, tc))
-            return carry
-
-        lax.fori_loop(first, last, body, 0)
+    def page_peer(j):
+        tx, ty, tc = peer(lax.rem(j * 37, GROUP))
+        return (tx * NY + ty) * NC + tc, at(tx, ty, tc)
+
+    def send_page(j):
+        number, target = page_peer(j)
+        send(arr.at[number], dec_mine, 0, target)
+
+    def arrange(j):
+        number, _ = page_peer(j)
+        for e in range(2):
+            page = jnp.maximum(jnp.minimum(inv[8 * e, number], GROUP - 1), 0)
+            for kv in range(2):
+                arr[number, kv, e] = paged[kv, e, page]
 
     def pages(n):
         first = 1 + sum(PAGES[:n])
-        send_pages(first, first + PAGES[n])
+        each(first, first + PAGES[n], 4, send_page)
 
     def other_chip(i):
         n = i + lax.div(i, 36)
@@ -134,9 +154,10 @@
             send(row, row, phase + 1, at(x, lax.rem(y + o, NY), c))
             send(column, column, phase + 1, at(lax.rem(x + o, NX), y, c))
 
-    def last_leg(buf, phase):
+    def last_leg(buf, phase, portion):
         take(rs_buf.at[pl.ds(0, 56)], rs.at[phase + 1])
         swap(buf, phase + 2)
+        pages(portion)
         take(buf.at[0], rs.at[phase + 2])
 
     def gone(buf, phase):
@@ -167,6 +188,43 @@
         inv_v[8 * e : 8 * e + 8, :] = dot_t(index, hits).astype(jnp.int32)
     to_scalars = pltpu.make_async_copy(inv_v, inv, own_sem.at[1])
     to_scalars.start()
+
+    copies[5].wait()
+    to_scalars.wait()
+
+    each(0, 1 + PAGES[0], 4, arrange)
+    fin[...] = jnp.zeros(fin.shape, BF16)
+    pl.semaphore_wait(barrier, GROUP - 1)
+
+    is_kv = lax.div(x, 4)
+    xx = lax.rem(x, 2)
+    ty4 = (1 - is_kv) * x + is_kv * (xx * 2 + lax.div(y, 4))
+    tc4 = (1 - is_kv) * lax.div(y, 4) + is_kv * lax.rem(lax.div(y, 2), 2)
+    slot = (1 - is_kv) * (lax.rem(y, 4) * 2 + c) + is_kv * (
+        8 + lax.div(lax.rem(x, 4), 2) * 4 + lax.rem(y, 2) * 2 + c
+    )
+
+    def send_heads(i, carry):
+        tx = lax.rem(x + lax.div(i, 2), NX)
+        ty = ty4 + 4 * lax.rem(i, 2)
+        same = (tx == x) & (ty == y) & (tc4 == c)
+
+        @pl.when(jnp.logical_not(same))
+        def _():
+            send(qs.at[lax.div(tx, 2)], qr.at[slot], 1, at(tx, ty, tc4))
+
+        @pl.when(same)
+        def _():
+            qr[slot] = qs[lax.div(tx, 2)]
+
+        return carry
+
+    lax.fori_loop(0, 16, send_heads, 0)
+    keeps_one = (lax.rem(y, 4) == ty4) & (tc4 == c)
+    own_copy = pltpu.make_async_copy(arr.at[me], dec_mine, own_sem.at[0])
+    own_copy.start()
+    pages(0)
+    each(1 + PAGES[0], GROUP, 4, arrange)
 
     copies[1].wait()
     slot_page = lax.broadcasted_iota(jnp.int32, (GROUP, GROUP * 8), 0)
@@ -184,47 +242,6 @@
         cosines.append(jnp.cos(angle))
         sines.append(jnp.where(lane < HEAD_DIM // 2, -sine, sine))
 
-    copies[5].wait()
-    to_scalars.wait()
-
-    def arrange(q, carry):
-        for e in range(2):
-            page = jnp.maximum(jnp.minimum(inv[8 * e, q], GROUP - 1), 0)
-            for kv in range(2):
-                arr[q, kv, e] = paged[kv, e, page]
-        return carry
-
-    lax.fori_loop(0, GROUP, arrange, 0, unroll=4)
-    pl.semaphore_wait(barrier, GROUP - 1)
-
-    is_kv = lax.div(x, 4)
-    xx = lax.rem(x, 2)
-    ty4 = (1 - is_kv) * x + is_kv * (xx * 2 + lax.div(y, 4))
-    tc4 = (1 - is_kv) * lax.div(y, 4) + is_kv * lax.rem(lax.div(y, 2), 2)
-    slot = (1 - is_kv) * (lax.rem(y, 4) * 2 + c) + is_kv * (
-        8 + lax.div(lax.rem(x, 4), 2) * 4 + lax.rem(y, 2) * 2 + c
-    )
-
-    def send_heads(i, carry):
-        tx = lax.rem(x + lax.div(i, 2), NX)
-        ty = ty4 + 4 * lax.rem(i, 2)
-        same = (tx == x) & (ty == y) & (tc4 == c)
-
-        @pl.when(jnp.logical_not(same))
-        def _():
-            send(qs.at[lax.div(tx, 2)], qr.at[slot], 1, at(tx, ty, tc4))
-
-        @pl.when(same)
-        def _():
-            qr[slot] = qs[lax.div(tx, 2)]
-
-        return carry
-
-    lax.fori_loop(0, 16, send_heads, 0)
-    keeps_one = (lax.rem(y, 4) == ty4) & (tc4 == c)
-    own_copy = pltpu.make_async_copy(arr.at[me], dec_mine, own_sem.at[0])
-    own_copy.start()
-    pages(0)
 
     @pl.when(keeps_one)
     def _():
@@ -279,7 +296,7 @@
     pages(1)
     second_leg(att_buf, 2)
     pages(2)
-    last_leg(att_buf, 2)
+    last_leg(att_buf, 2, 3)
 
     want = lax.broadcasted_iota(jnp.int32, (128, 256), 0)
     have = lax.broadcasted_iota(jnp.int32, (128, 256), 1)
@@ -308,15 +325,15 @@
     mix_buf[c, x2, xp, y2, yp] = (dot_n(mixed_part[:16], put0) + dot_n(mixed_part[16:], put1)).astype(BF16)
 
     first_leg(mix_buf, 5)
-    pages(3)
+    pages(4)
     for k in range(PREFILL_TP):
         picked = dot_n(pick_kv, by_slot(k)).astype(BF16)
         for a in range(2):
             nk_ref[:, pl.ds((2 * k + a) * TILE, TILE)] = picked[32 * a : 32 * a + 32]
             nv_ref[:, pl.ds((2 * k + a) * TILE, TILE)] = picked[64 + 32 * a : 96 + 32 * a]
     second_leg(mix_buf, 5)
-    pages(4)
-    last_leg(mix_buf, 5)
+    pages(5)
+    last_leg(mix_buf, 5, 6)
 
     lane16 = lax.broadcasted_iota(jnp.int32, (16, TILE), 1)
 
@@ -362,7 +379,7 @@
     take(pr, rs.at[8])
     sb[...] = (br[c].astype(F32) + pr[...].astype(F32)).astype(BF16)
 
-    def send_sums(j, carry):
+    def send_sums(j):
         owner = lax.div(j * 16, 9)
         tile = sb.at[:, pl.ds(pl.multiple_of(j * TILE, TILE), TILE)]
 
@@ -374,12 +391,17 @@
         def _():
             rs_buf[chip] = tile[...]
 
-        return carry
-
-    lax.fori_loop(0, TILES, send_sums, 0)
-    pages(5)
+    each(0, TILES, 6, send_sums)
+    pages(7)
     my_tile = lax.div(chip * 9 + 15, 16)
     owns = lax.div(my_tile * 16, 9) == chip
+    chip_cols = NC * COLS
+    last_reader = lax.div(my_tile * TILE + TILE - 1, chip_cols)
+    low = lax.div(chip * chip_cols, TILE)
+    high = lax.div(chip * chip_cols + chip_cols - 1, TILE)
+    low_tile = jnp.minimum(low, TILES - 2)
+    needs_low = lax.div(low * 16, 9) != chip
+    needs_high = (high != low) & (lax.div(high * 16, 9) != chip)
 
     @pl.when(owns)
     def _():
@@ -391,40 +413,55 @@
                 acc = acc + rs_buf[i * 8 + n].astype(F32)
             return acc
 
-        fin[c, my_tile] = lax.fori_loop(0, 8, add, total).astype(BF16)
-
-        def tell(i, carry):
+        total = lax.fori_loop(0, 8, add, total)
+        fin[c, my_tile] = total.astype(BF16)
+        squares = jnp.sum(total * total, axis=1, keepdims=True)
+        sqs[c, my_tile] = jnp.sum(jnp.where(rows16 == lane16, squares, 0.0), axis=0, keepdims=True)
+        for ahead in (1, 2):
+
+            @pl.when(chip + ahead <= last_reader)
+            def _():
+                reader = chip + ahead
+                send(fin.at[c, my_tile], fin.at[c, my_tile], 12, at(lax.div(reader, NY), lax.rem(reader, NY), c))
+
+        def tell(i):
             tx, ty = other_chip(i)
-            send(fin.at[c, my_tile], fin.at[c, my_tile], 10, at(tx, ty, c))
-            return carry
-
-        lax.fori_loop(0, CHIPS - 1, tell, 0)
-
-    pages(6)
+            send(sqs.at[c, my_tile], sqs.at[c, my_tile], 10, at(tx, ty, c))
+
+        each(0, CHIPS - 1, 9, tell)
+
+    pages(8)
 
     @pl.when(owns)
     def _():
-        take(fin.at[0, pl.ds(0, TILES - 1)], rs.at[10])
+        take(sqs.at[0, pl.ds(0, TILES - 1)], rs.at[10])
 
     @pl.when(jnp.logical_not(owns))
     def _():
-        take(fin.at[0, pl.ds(0, TILES)], rs.at[10])
-
-    swap(fin, 11)
-    take(fin.at[0], rs.at[11])
+        take(sqs.at[0, pl.ds(0, TILES)], rs.at[10])
+
+    @pl.when(needs_low & needs_high)
+    def _():
+        take(fin.at[0, pl.ds(0, 2)], rs.at[12])
+
+    @pl.when(needs_low != needs_high)
+    def _():
+        take(fin.at[0, pl.ds(0, 1)], rs.at[12])
+
+    swap(sqs, 11)
+    send(fin.at[c, pl.ds(low_tile, 2)], fin.at[c, pl.ds(low_tile, 2)], 13, at(x, y, 1 - c))
+    take(sqs.at[0], rs.at[11])
+    take(fin.at[0, pl.ds(0, 2)], rs.at[13])
 
     first = lax.div(me * COLS, TILE)
     second = jnp.minimum(first + 1, TILES - 1)
     for half in range(2):
 
-        def square(j, acc):
-            for n in range(4):
-                tile = fin[half, j * 4 + n].astype(F32)
-                acc = acc + tile * tile
-            return acc
-
-        squares = lax.fori_loop(0, TILES // 4, square, jnp.zeros((16, TILE), F32))
-        factor = lax.rsqrt(jnp.sum(squares, axis=1, keepdims=True) / D + EPSILON)
+        squares = jnp.zeros((1, TILE), F32)
+        for t in range(TILES):
+            squares = squares + sqs[half, t]
+        by_row = jnp.where(rows16 == lane16, jnp.broadcast_to(squares, (16, TILE)), 0.0)
+        factor = lax.rsqrt(jnp.sum(by_row, axis=1, keepdims=True) / D + EPSILON)
 
         def block(t):
             columns = pl.ds(pl.multiple_of(t * TILE, TILE), TILE)
@@ -453,13 +490,22 @@
     @pl.when(owns)
     def _():
         take(fin.at[0, pl.ds(0, TILES - 1)], ss.at[9])
-        take(rs_buf.at[pl.ds(0, CHIPS - 1)], ss.at[10])
+        take(marks, ss.at[10])
+
+        @pl.when(chip + 2 <= last_reader)
+        def _():
+            take(fin.at[0, pl.ds(0, 2)], ss.at[12])
+
+        @pl.when((chip + 1 <= last_reader) & (chip + 2 > last_reader))
+        def _():
+            take(fin.at[0, pl.ds(0, 1)], ss.at[12])
 
     @pl.when(jnp.logical_not(owns))
     def _():
         take(fin.at[0, pl.ds(0, TILES)], ss.at[9])
 
-    take(fin.at[0], ss.at[11])
+    take(sqs.at[0], ss.at[11])
+    take(fin.at[0, pl.ds(0, 2)], ss.at[13])
 
 
 def on_device(
@@ -523,10 +569,12 @@
             pltpu.VMEM((16, D), BF16),
             pltpu.VMEM((CHIPS, 16, TILE), BF16),
             pltpu.VMEM((NC, TILES, 16, TILE), BF16),
+            pltpu.VMEM((NC, TILES, 1, TILE), F32),
+            pltpu.VMEM((CHIPS - 1, 1, TILE), F32),
             dma((10,)),
             dma((2,)),
-            dma((12,)),
-            dma((12,)),
+            dma((14,)),
+            dma((14,)),
         ],
         compiler_params=pltpu.CompilerParams(
             collective_id=0, has_side_effects=True, vmem_limit_bytes=48 * 2**20

time: 107 us -> 106 us (level); the launches traced: 107 us -> 104 us
  Pallas kernels: 103 us -> 100 us
    pallas_call x1, Pallas kernels: 103 us -> 100 us  [on_device(): pl.pallas_call(step_kernel, name='step', out_shape=(jax.ShapeDtypeStruct(...]
where the time goes in v4:
time: 106 us; the launch traced here: 104 us
  Pallas kernels  100 us (94%)
  other arithmetic  2.41 us (2%)
    pallas_call x1, Pallas kernels, on_device(): pl.pallas_call(step_kernel, name='step', out_shape=(jax.ShapeDtypeStruct(...  100 us

profile of v4, /device:TPU:513, one launch (start us, length us, event | category | flops | bytes accessed | tf_op | source)
XLA Modules:
  0.0 104.0 jit_solution(13461360236826037130)
XLA Ops:
  0.6 0.7 broadcast_compare_fusion
  1.4 100.3 %step.1 = (f32[32,128]{1,0:T(8,128)S(1)}, bf16[32,2048]{1,0:T(8,128)(2,1)S(1)}, bf16[32,2048]{1,0:T(8,128)(2,1)S(1)}, bf16[1,1,2,32,8,2048]{5,4,3,2,1,0:T(8,128)(2,1)S(1)}) custom-call(s32[32]{0:T(128)} %len_ref.1, s32[32,128]{1,0:T(8,128)} %table_hbm.1, f32[1,128]{1,0:T(1,128)} %constant.20.clone.freq_hbm, f32[32,4608]{1,0:T(8,128)} %hid_hbm.1, ...), custom_call_target="tpu_custom_call" | custom-call | tf_op jit(solution)/shard_map/step/pallas_call | solution.py:534
  101.7 1.6 %broadcast_select_fusion = bf16[1,1,2,32,8,2048]{5,4,3,2,1,0:T(8,128)(2,1)} fusion(bf16[1,1,2,32,8,2048]{5,4,3,2,1,0:T(8,128)(2,1)S(1)} %get-tuple-element.9, pred[32,8]{1,0:T(8,128)(4,1)S(1)} %broadcast_compare_fusion, bf16[2,32,2048]{2,1,0:T(8,128)(2,1)S(1)} %pad_maximum_fusion), kind=kLoop, calls=%fused_computation | loop fusion | flops 1048576 | bytes 4456704 | tf_op jit(solution)/shard_map/jit(_where)/select_n | solution.py:594
  103.4 0.6 copy.13
  (2 shorter events, 0.0 us)

commit v5 on v4

--- a/solution.py
+++ b/solution.py
@@ -48,7 +48,7 @@
 
 def step_kernel(
     len_ref, table_hbm, freq_hbm, hid_hbm, paged_hbm, cache_hbm, wq_hbm, wo_hbm, wg_hbm, wd_hbm, gain_hbm,
-    res_ref, nk_ref, nv_ref, dec_ref,
+    res_ref, nk_ref, nv_ref, fresh_ref, dec_ref,
     table, freq, inv_v, inv, hid, paged, cache, wq, wo, wg, wd, gain, arr, qs, qr, qf, att_buf, att, mix_buf, mix, stream,
     br, pr, sb, rs_buf, fin, sqs, marks, in_sem, own_sem, ss, rs,
 ):
@@ -111,7 +111,7 @@
     dec_mine = dec_ref.at[0, 0, :, pl.ds(my_group * 2, 2), :, pl.ds(pl.multiple_of(my_slot * 256, 256), 256)]
 
     def page_peer(j):
-        tx, ty, tc = peer(lax.rem(j * 37, GROUP))
+        tx, ty, tc = peer(lax.rem(j * 53, GROUP))
         return (tx * NY + ty) * NC + tc, at(tx, ty, tc)
 
     def send_page(j):
@@ -326,6 +326,12 @@
 
     first_leg(mix_buf, 5)
     pages(4)
+    request = lax.broadcasted_iota(jnp.int32, fresh_ref.shape, 0)
+    place = me * 8 + lax.broadcasted_iota(jnp.int32, fresh_ref.shape, 1)
+    position = jnp.zeros(fresh_ref.shape, jnp.int32)
+    for r in range(fresh_ref.shape[0]):
+        position = jnp.where(request == r, len_ref[r], position)
+    fresh_ref[...] = jnp.where(position == place, 1, 0)
     for k in range(PREFILL_TP):
         picked = dot_n(pick_kv, by_slot(k)).astype(BF16)
         for a in range(2):
@@ -469,7 +475,8 @@
             value = stream[16 * half : 16 * half + 16, columns] + branch * factor * (1.0 + gain[3:4, columns])
             return pltpu.roll(value, lax.rem(TILE - shift, TILE), 1)
 
-        res_ref[16 * half : 16 * half + 16, :] = jnp.where(lane16 < TILE - shift, block(first), block(second))
+        value = jnp.where(lane16 < TILE - shift, block(first), block(second))
+        res_ref[16 * half : 16 * half + 16, :] = value[:, :COLS]
 
     own_copy.wait()
     take(arr.at[pl.ds(0, GROUP - 1)], rs.at[0])
@@ -519,7 +526,6 @@
     down_weight,
     norm_gains,
 ):
-    me = lax.axis_index(TP)
     batch = hidden_in.shape[0]
     page_width = prefill_cache.shape[5]
     exponent = np.arange(HEAD_DIM // 2, dtype=np.float32) * np.float32(-2.0 / HEAD_DIM)
@@ -531,17 +537,18 @@
     vmem = pl.BlockSpec(memory_space=pltpu.VMEM)
     hbm = pl.BlockSpec(memory_space=pltpu.HBM)
     dma = pltpu.SemaphoreType.DMA
-    res, new_key, new_value, decoded = pl.pallas_call(
+    res, new_key, new_value, fresh, decoded = pl.pallas_call(
         step_kernel,
         name="step",
         out_shape=(
-            jax.ShapeDtypeStruct((batch, TILE), F32),
+            jax.ShapeDtypeStruct((batch, COLS), F32),
             jax.ShapeDtypeStruct((batch, k_cols), BF16),
             jax.ShapeDtypeStruct((batch, k_cols), BF16),
+            jax.ShapeDtypeStruct((batch, page_width), jnp.int32),
             jax.ShapeDtypeStruct((1, 1, 2, batch, page_width, k_cols), BF16),
         ),
         in_specs=[pl.BlockSpec(memory_space=pltpu.SMEM)] + [hbm] * 10,
-        out_specs=(vmem, vmem, vmem, pl.BlockSpec(memory_space=pl.ANY)),
+        out_specs=(vmem, vmem, vmem, vmem, pl.BlockSpec(memory_space=pl.ANY)),
         scratch_shapes=[
             pltpu.VMEM(page_table.shape, jnp.int32),
             pltpu.VMEM(frequency.shape, F32),
@@ -588,11 +595,10 @@
             )
         ]
     )
-    my_pos = me * page_width + jnp.arange(page_width, dtype=jnp.int32)
-    fresh = (my_pos[None, :] == lengths[:, None])[None, None, None, :, :, None]
+    fresh = (fresh != 0)[None, None, None, :, :, None]
     new = jnp.stack([new_key, new_value], axis=0).reshape(1, 1, 2, batch, 1, k_cols)
     decode_cache = jnp.where(fresh, new, decoded)
-    return (res[:, :COLS], decode_cache)
+    return (res, decode_cache)
 
 
 def solution(mesh):

time: 106 us -> 103 us (0.972); the launches traced: 104 us -> 103 us
  no operation moved by 1% of the time
where the time goes in v5:
time: 103 us
  Pallas kernels  100 us (97%)
  other arithmetic  1.68 us (2%)
    pallas_call x1, Pallas kernels, on_device(): pl.pallas_call(step_kernel, name='step', out_shape=(jax.ShapeDtypeStruct(...  100 us

profile of v5, /device:TPU:513, one launch (start us, length us, event | category | flops | bytes accessed | tf_op | source)
XLA Modules:
  0.0 102.9 jit_solution(8951429604465085029)
XLA Ops:
  0.6 100.0 %step.1 = (f32[32,36]{1,0:T(8,128)S(1)}, bf16[32,2048]{1,0:T(8,128)(2,1)S(1)}, bf16[32,2048]{1,0:T(8,128)(2,1)S(1)}, s32[32,8]{1,0:T(8,128)S(1)}, bf16[1,1,2,32,8,2048]{5,4,3,2,1,0:T(8,128)(2,1)S(1)}) custom-call(s32[32]{0:T(128)} %len_ref.1, s32[32,128]{1,0:T(8,128)} %table_hbm.1, f32[1,128]{1,0:T(1,128)} %constant.4.clone.freq_hbm, f32[32,4608]{1,0:T(8,128)} %hid_hbm.1, ...), custom_call_target="tpu_custom_call" | custom-call | tf_op jit(solution)/shard_map/step/pallas_call | solution.py:540
  100.7 1.6 %broadcast_select_fusion = bf16[1,1,2,32,8,2048]{5,4,3,2,1,0:T(8,128)(2,1)} fusion(bf16[1,1,2,32,8,2048]{5,4,3,2,1,0:T(8,128)(2,1)S(1)} %get-tuple-element.11, pred[32,8]{1,0:T(8,128)(4,1)S(1)} %broadcast_compare_fusion, bf16[2,32,2048]{2,1,0:T(8,128)(2,1)S(1)} %pad_maximum_fusion), kind=kLoop, calls=%fused_computation | loop fusion | flops 1048576 | bytes 4456704 | tf_op jit(solution)/shard_map/jit(_where)/select_n | solution.py:600
  102.3 0.6 copy.13
  (2 shorter events, 0.0 us)

commit v6 on v5

--- a/solution.py
+++ b/solution.py
@@ -72,8 +72,16 @@
         tc = lax.rem(c + lax.rem(i, NC), NC)
         return tx, ty, tc
 
-    def greet(i, carry):
-        pl.semaphore_signal(barrier, inc=1, device_id=at(*peer(i)), device_id_type=MESH)
+    all_y = [lax.rem(y + n, NY) for n in (4, 3, 5, 2, 6, 1, 7, 0)]
+
+    def greet(tx, ty, tc):
+        pl.semaphore_signal(barrier, inc=1, device_id=at(tx, ty, tc), device_id_type=MESH)
+
+    def greet_row(n, carry):
+        tx = lax.rem(x + 1 + n, NX)
+        for ty in all_y:
+            greet(tx, ty, c)
+            greet(tx, ty, 1 - c)
         return carry
 
     loads = [
@@ -84,7 +92,11 @@
     copies = [pltpu.make_async_copy(s, d, in_sem.at[n]) for n, (s, d) in enumerate(loads)]
     for copy in copies:
         copy.start()
-    lax.fori_loop(1, GROUP, greet, 0)
+    lax.fori_loop(0, NX - 1, greet_row, 0)
+    for ty in all_y[:-1]:
+        greet(x, ty, c)
+        greet(x, ty, 1 - c)
+    greet(x, y, 1 - c)
 
     def send(src, dst, phase, target):
         pltpu.make_async_remote_copy(

time: 103 us -> 104 us (level)
    pallas_call x1, Pallas kernels: 100 us -> 101 us  [on_device(): pl.pallas_call(step_kernel, name='step', out_shape=(jax.ShapeDtypeStruct(...]
where the time goes in v6:
time: 104 us
  Pallas kernels  101 us (97%)
  other arithmetic  1.68 us (2%)
    pallas_call x1, Pallas kernels, on_device(): pl.pallas_call(step_kernel, name='step', out_shape=(jax.ShapeDtypeStruct(...  101 us

profile of v6, /device:TPU:513, one launch (start us, length us, event | category | flops | bytes accessed | tf_op | source)
XLA Modules:
  0.0 104.1 jit_solution(150463059980259464)
XLA Ops:
  0.6 101.2 %step.1 = (f32[32,36]{1,0:T(8,128)S(1)}, bf16[32,2048]{1,0:T(8,128)(2,1)S(1)}, bf16[32,2048]{1,0:T(8,128)(2,1)S(1)}, s32[32,8]{1,0:T(8,128)S(1)}, bf16[1,1,2,32,8,2048]{5,4,3,2,1,0:T(8,128)(2,1)S(1)}) custom-call(s32[32]{0:T(128)} %len_ref.1, s32[32,128]{1,0:T(8,128)} %table_hbm.1, f32[1,128]{1,0:T(1,128)} %constant.4.clone.freq_hbm, f32[32,4608]{1,0:T(8,128)} %hid_hbm.1, ...), custom_call_target="tpu_custom_call" | custom-call | tf_op jit(solution)/shard_map/step/pallas_call | solution.py:552
  101.8 1.6 %broadcast_select_fusion = bf16[1,1,2,32,8,2048]{5,4,3,2,1,0:T(8,128)(2,1)} fusion(bf16[1,1,2,32,8,2048]{5,4,3,2,1,0:T(8,128)(2,1)S(1)} %get-tuple-element.11, pred[32,8]{1,0:T(8,128)(4,1)S(1)} %broadcast_compare_fusion, bf16[2,32,2048]{2,1,0:T(8,128)(2,1)S(1)} %pad_maximum_fusion), kind=kLoop, calls=%fused_computation | loop fusion | flops 1048576 | bytes 4456704 | tf_op jit(solution)/shard_map/jit(_where)/select_n | solution.py:612
  103.5 0.6 copy.13
  (2 shorter events, 0.0 us)
